TPU v7x, 32 devices: a whole 2x2x4 slice. The times are simulated.
32 devices in a mesh: cls: 8 (over z, y), row: 4 (over x, core).
Axes of the slice: x: 2, y: 2, z: 4, core: 2. Of those that a mesh axis runs over, the one named last changes fastest.
Arguments:
- embeddings: float32 [1024, 1024], P('row'), may hold values from -6 to 6
- weights: float32 [1024, 81920], P(('cls', 'row')), may hold values from -4 to 4
- labels: int32 [1024], replicated, may hold values from 0 to 81919, as said below
Outputs:
- weight_update: float32 [1024, 81920], P(None, ('cls', 'row'))
- losses: float32 [2, 1024], replicated
Inputs may be any that keep to these rules, and one draw needn't show every extreme that they name: labels take at most 512 distinct values, at most one in each aligned run of 160 classes; rows may share a label.
All inputs are finite; a program needn't handle non-finite values.
Results may differ from a plain program's by a relative error of at most 0.012.
The roundings to bfloat16 on the way count: a program that leaves them out, or rounds other values in their place, can miss the bound.
Values may be sent and summed in bfloat16 or wider, within the bound.
No kernel may reach another device: no remote copies, remote signals or barrier semaphores. Data moves between devices by JAX's collectives and lax.ppermute only.
A program may use at most 128 MiB of HBM per device.

v0:
```python
import jax
import jax.numpy as jnp
from jax import lax
from jax.sharding import PartitionSpec as P

STEPS = 2


learn_rate = 2.0


def shards(embeddings, weights, labels):
    peer_count = lax.axis_size(("cls", "row"))
    examples = lax.all_gather(embeddings.astype(jnp.bfloat16), "row", axis=0, tiled=True)
    row_count = examples.shape[0]
    feature_rows = weights.shape[0]
    class_count = weights.shape[1] // peer_count
    model_width = feature_rows * peer_count
    offset = lax.axis_index(("cls", "row")) * class_count
    columns = lax.broadcasted_iota(jnp.int32, (1, class_count), 1) + offset
    label_hit = columns == labels[:, None]
    pieces = weights.reshape(feature_rows, peer_count, class_count // 128, 128)
    block_weights = lax.all_to_all(pieces, ("cls", "row"), split_axis=1, concat_axis=0, tiled=True)[
        :, 0
    ]
    block_width = block_weights.shape[1] * 128
    flat_weights = block_weights.reshape(block_weights.shape[0], block_width)
    block_logits = jnp.dot(
        examples, flat_weights.astype(jnp.bfloat16), preferred_element_type=jnp.float32
    )
    first_logits = block_logits.reshape(row_count, block_weights.shape[1], 128)
    current = block_weights.reshape(model_width, class_count)
    logits = first_logits.reshape(row_count, class_count)
    starting = current
    loss_rows = []
    for step_index in range(STEPS):
        if step_index > 0:
            logits = jnp.dot(
                examples, current.astype(jnp.bfloat16), preferred_element_type=jnp.float32
            )
        local_peak = jnp.max(logits, axis=1)
        local_picked = jnp.sum(jnp.where(label_hit, logits, 0.0), axis=1)
        row_peak = lax.pmax(local_peak, ("cls", "row"))
        row_total, picked = lax.psum(
            (jnp.sum(jnp.exp(logits - row_peak[:, None]), axis=1), local_picked), ("cls", "row")
        )
        log_norm = row_peak + jnp.log(row_total)
        loss_rows.append(log_norm - picked)
        onehot = jnp.where(label_hit, 1.0, 0.0)
        residual = (jnp.exp(logits - log_norm[:, None]) - onehot).astype(jnp.bfloat16)
        gradient = (
            lax.dot_general(
                examples, residual, (((0,), (0,)), ((), ())), preferred_element_type=jnp.float32
            )
            / row_count
        )
        current = current - learn_rate * gradient
    return (current - starting, jnp.stack(loss_rows))


def solution(mesh):
    placed = (P("row", None), P(("cls", "row"), None), P())
    return jax.shard_map(
        shards,
        mesh=mesh,
        in_specs=placed,
        out_specs=(P(None, ("cls", "row")), P()),
        check_vma=False,
    )
```

profile of v0, /device:TPU:0, one launch (start us, length us, event | category | flops | bytes accessed | tf_op | source)
XLA Modules:
  0.0 568.5 jit_solution(8699041707677321800)
XLA Ops:
  7.2 9.4 %reshape.18 = f32[32,32,20,128]{3,2,1,0:T(8,128)} reshape(f32[32,81920]{1,0:T(8,128)} %param.4) | data formatting | bytes 20971520 | tf_op jit(solution)/shard_map/reshape | solution.py:22
  16.6 14.7 %copy.13 = f32[32,32,20,128]{3,0,2,1:T(8,128)} copy(f32[32,32,20,128]{3,2,1,0:T(8,128)} %reshape.18) | data formatting | bytes 20971520 | tf_op jit(solution)/shard_map/reshape | solution.py:22
  31.3 0.0 copy-start
  31.3 7.4 %all-to-all-start = ((f32[32,32,20,128]{3,0,2,1:T(8,128)}), f32[32,32,20,128]{3,0,2,1:T(8,128)}, u32[]{:S(2)}, u32[]{:S(2)}) async-start(f32[32,32,20,128]{3,0,2,1:T(8,128)} %copy.13), calls=%async_computation | async-start | bytes 20971520 | tf_op jit(solution)/shard_map/all_to_all | solution.py:23
  38.8 0.2 all-gather.2.cloned.1.call-start
  39.0 0.0 copy-done
  39.0 0.9 convert_element_type.15
  39.9 0.0 all-gather.2.cloned.1.call-update
  39.9 234.8 %all-to-all-done = f32[32,32,20,128]{3,0,2,1:T(8,128)} async-done(((f32[32,32,20,128]{3,0,2,1:T(8,128)}), f32[32,32,20,128]{3,0,2,1:T(8,128)}, u32[]{:S(2)}, u32[]{:S(2)}) %all-to-all-start) | async-done | bytes 10485792 | tf_op jit(solution)/shard_map/all_to_all | solution.py:23
  274.7 17.8 %copy.14 = f32[32,32,1,20,128]{4,3,1,0,2:T(8,128)} copy(f32[32,32,1,20,128]{4,1,3,0,2:T(8,128)} %bitcast.1) | data formatting | bytes 20971520 | tf_op jit(solution)/shard_map/all_to_all | solution.py:23
  292.5 11.4 %copy.21 = f32[128,8,20,128]{3,1,2,0:T(8,128)} copy(f32[128,8,20,128]{3,2,1,0:T(8,128)} %bitcast.41) | data formatting | bytes 20971520
  303.9 11.4 %copy.15 = f32[1024,2560]{0,1:T(8,128)} copy(f32[1024,2560]{1,0:T(8,128)} %bitcast.42) | data formatting | bytes 20971520 | tf_op jit(solution)/shard_map/reshape;squeeze | solution.py:32
  315.3 0.0 copy-start.1
  315.3 0.0 all-gather.2.cloned.1.call-done
  315.3 11.4 %fusion.35 = (f32[1024]{0:T(1024)S(1)}, f32[1024,2560]{1,0:T(8,128)}) fusion(bf16[1024,1024]{1,0:T(8,128)(2,1)} %all-gather.2.cloned.1.call-done, f32[1024,2560]{1,0:T(8,128)} %bitcast.43), kind=kOutput, calls=%fused_computation.45 | convolution fusion | flops 5373950976 | bytes 23072768 | tf_op jit(solution)/shard_map/dot_general | solution.py:28
  326.6 36.8 %pmax.14 = f32[1024]{0:T(1024)S(1)} all-reduce(f32[1024]{0:T(1024)S(1)} %get-tuple-element.17), channel_id=1, replica_groups=mesh['cls'=8,'row'=4] {'cls','row'}, use_global_device_ids=true, to_apply=%region_1.2 | all-reduce | flops 1024 | bytes 8192 | tf_op jit(solution)/shard_map/pmax | solution.py:43
  363.5 0.0 copy-done.1
  363.5 0.0 slice-start
  363.5 5.7 %fusion.4 = (f32[1024]{0:T(1024)S(1)}, f32[1024]{0:T(1024)S(1)}) fusion(f32[1024,2560]{1,0:T(8,128)} %get-tuple-element.18, s32[2560]{0:T(1024)S(1)} %iota_add_fusion, s32[1024]{0:T(1024)S(1)} %copy-done.1, f32[1024]{0:T(1024)S(1)} %pmax.14), kind=kLoop, calls=%fused_computation.7 | loop fusion | flops 13105152 | bytes 10512384 | tf_op jit(solution)/shard_map/reduce_sum | solution.py:42
  369.2 41.0 %psum.28 = f32[1024]{0:T(1024)S(1)} all-reduce(f32[1024]{0:T(1024)S(1)} %get-tuple-element.9), channel_id=1, replica_groups=mesh['cls'=8,'row'=4] {'cls','row'}, use_global_device_ids=true, to_apply=%region_3.4 | all-reduce | flops 1024 | bytes 8192 | tf_op jit(solution)/shard_map/psum | solution.py:44
  410.2 0.0 slice-start.1
  410.2 0.0 slice-start.2
  410.2 0.0 copy-start.2
  410.2 12.0 %fusion.14 = f32[2560,1024]{1,0:T(8,128)} fusion(bf16[1024,1024]{1,0:T(8,128)(2,1)} %all-gather.2.cloned.1.call-done, f32[1024,2560]{1,0:T(8,128)} %get-tuple-element.18, s32[2560]{0:T(1024)S(1)} %iota_add_fusion, f32[1024]{0:T(1024)S(1)} %log_add_fusion.1, s32[1024]{0:T(1024)S(1)} %copy-done.1), kind=kOutput, calls=%fused_computation.21 | convolution fusion | flops 5381816320 | bytes 23087104 | tf_op jit(solution)/shard_map/dot_general | solution.py:52
  422.2 0.0 slice-done
  422.2 0.0 slice-done.1
  422.2 0.0 slice-done.2
  422.3 0.0 copy-done.2
  422.3 12.4 %fusion.36 = (f32[1024]{0:T(1024)S(1)}, f32[2560,1024]{1,0:T(8,128)}) fusion(bf16[1024,1024]{1,0:T(8,128)(2,1)S(1)} %copy-done.2, f32[1024,2560]{0,1:T(8,128)S(1)} %bitcast.45, f32[2560,1024]{1,0:T(8,128)} %fusion.14), kind=kOutput, calls=%fused_computation.46 | convolution fusion | flops 5379193856 | bytes 33558528 | tf_op jit(solution)/shard_map/dot_general | solution.py:38
  434.6 39.6 %pmax.15 = f32[1024]{0:T(1024)S(1)} all-reduce(f32[1024]{0:T(1024)S(1)} %get-tuple-element.19), channel_id=1, replica_groups=mesh['cls'=8,'row'=4] {'cls','row'}, use_global_device_ids=true, to_apply=%region_5.6 | all-reduce | flops 1024 | bytes 8192 | tf_op jit(solution)/shard_map/pmax | solution.py:43
  474.3 11.5 %copy.16 = f32[2560,1024]{0,1:T(8,128)} copy(f32[2560,1024]{1,0:T(8,128)} %get-tuple-element.20) | data formatting | bytes 20971520 | tf_op jit(solution)/shard_map/dot_general | solution.py:38
  485.8 5.6 fusion.5
  491.4 40.7 %all-reduce = (f32[1024]{0:T(1024)S(1)}, f32[1024]{0:T(1024)S(1)}, f32[1024]{0:T(1024)S(1)}) all-reduce(f32[1024]{0:T(1024)S(1)} %get-tuple-element.11, f32[1024]{0:T(1024)S(1)} %get-tuple-element.10, f32[1024]{0:T(1024)S(1)} %get-tuple-element.8), channel_id=1, replica_groups=mesh['cls'=8,'row'=4] {'cls','row'}, use_global_device_ids=true, to_apply=%region_7.8 | all-reduce | flops 3072 | bytes 24576 | tf_op jit(solution)/shard_map/psum | solution.py:44
  532.1 17.2 %fusion.6 = f32[1024,2560]{0,1:T(8,128)} fusion(f32[1024,2560]{0,1:T(8,128)} %copy.15, f32[2560,1024]{1,0:T(8,128)} %fusion.14, bf16[1024,1024]{1,0:T(8,128)(2,1)} %all-gather.2.cloned.1.call-done, f32[2560,1024]{0,1:T(8,128)} %copy.16, f32[1024]{0:T(1024)S(1)} %get-tuple-element.16, s32[2560]{0:T(1024)S(1)} %iota_add_fusion, s32[1024]{0:T(1024)S(1)} %copy-done.1), kind=kOutput, calls=%fused_computation.11 | convolution fusion | flops 5394923520 | bytes 44058624 | tf_op jit(solution)/shard_map/dot_general | solution.py:52
  549.2 11.4 %copy.18 = f32[1024,2560]{1,0:T(8,128)} copy(f32[1024,2560]{0,1:T(8,128)} %fusion.6) | data formatting | bytes 20971520
  560.6 0.6 pad_maximum_fusion
  (5 shorter events, 0.0 us)
Async XLA Ops:
  31.3 7.7 %copy-start = (f32[256,1024]{1,0:T(8,128)S(1)}, f32[256,1024]{1,0:T(8,128)}, u32[]{:S(2)}) copy-start(f32[256,1024]{1,0:T(8,128)} %param.3) | copy-start | bytes 3145732
  31.3 243.4 %all-to-all-start = ((f32[32,32,20,128]{3,0,2,1:T(8,128)}), f32[32,32,20,128]{3,0,2,1:T(8,128)}, u32[]{:S(2)}, u32[]{:S(2)}) async-start(f32[32,32,20,128]{3,0,2,1:T(8,128)} %copy.13), calls=%async_computation | async-start | bytes 20971520 | tf_op jit(solution)/shard_map/all_to_all | solution.py:23
  38.8 276.5 %all-gather.2.cloned.1.call-start = ((), (), s32[]{:S(2)}) async-start(), calls=%async_computation.1 | async-start | bytes 2621440 | tf_op jit(solution)/shard_map/all_gather | solution.py:14
  315.3 48.2 %copy-start.1 = (s32[1024]{0:T(1024)S(1)}, s32[1024]{0:T(1024)}, u32[]{:S(2)}) copy-start(s32[1024]{0:T(1024)} %param.5) | copy-start | bytes 12292
  363.5 58.8 %slice-start = ((s8[10485760]{0:T(1024)(128)(4,1)}), s8[2097152]{0:T(1024)(128)(4,1)S(1)}, s32[]{:S(2)}) async-start(s8[10485760]{0:T(1024)(128)(4,1)} %bitcast.44), calls=%async_computation.2 | async-start | bytes 4194304
  410.2 12.0 %slice-start.1 = ((s8[10485760]{0:T(1024)(128)(4,1)}), s8[4194304]{0:T(1024)(128)(4,1)S(1)}, s32[]{:S(2)}) async-start(s8[10485760]{0:T(1024)(128)(4,1)} %bitcast.44), calls=%async_computation.3 | async-start | bytes 8388608
  410.2 12.0 %slice-start.2 = ((s8[10485760]{0:T(1024)(128)(4,1)}), s8[4194304]{0:T(1024)(128)(4,1)S(1)}, s32[]{:S(2)}) async-start(s8[10485760]{0:T(1024)(128)(4,1)} %bitcast.44), calls=%async_computation.4 | async-start | bytes 8388608
  410.2 12.0 %copy-start.2 = (bf16[1024,1024]{1,0:T(8,128)(2,1)S(1)}, bf16[1024,1024]{1,0:T(8,128)(2,1)}, u32[]{:S(2)}) copy-start(bf16[1024,1024]{1,0:T(8,128)(2,1)} %all-gather.2.cloned.1.call-done) | copy-start | bytes 6291460
Sparse Core Ops, SparseCore 0:
  41.1 74.9 all-gather.1
where the time goes:
time: 575 us; the launch traced here: 569 us
  waiting for transfers between devices  235 us (41%)
  blocking collectives  158 us (27%)
  local copies, waits for them, and re-layouts  87.6 us (15%)
  matrix products  52.9 us (9%)
  between operations  14.6 us (3%)
  other arithmetic  12.8 us (2%)
  starting transfers between devices  7.65 us (1%)
    all_to_all x1, waiting for transfers between devices, shards(): lax.all_to_all(pieces, ('cls', 'row'), split_axis=1, concat_axis=0, tiled...  235 us
    psum x2, blocking collectives, shards(): lax.psum((jnp.sum(jnp.exp(logits - row_peak[:, None]), axis=1), local_pic...  81.7 us
    pmax x2, blocking collectives, shards(): row_peak = lax.pmax(local_peak, ('cls', 'row'))  76.5 us
    dot_general x2, matrix products, shards(): lax.dot_general(examples, residual, (((0,), (0,)), ((), ())), preferred_e...  29.2 us
    reshape x2, local copies, waits for them, and re-layouts, shards(): pieces = weights.reshape(feature_rows, peer_count, class_count // 128, 128)  24.2 us
    unnamed x14, local copies, waits for them, and re-layouts  22.8 us
    all_to_all x1, local copies, waits for them, and re-layouts, shards(): lax.all_to_all(pieces, ('cls', 'row'), split_axis=1, concat_axis=0, tiled...  17.8 us
    dot_general x1, matrix products, shards(): jnp.dot(examples, current.astype(jnp.bfloat16), preferred_element_type=jn...  12.4 us
  transfers between devices with their start and end apart: 2, of which 1 were waited for; matrix products, arithmetic and copies ran while one was open for 7% of the time, Pallas kernels for 0%

commit v1 on v0

v1 whole, which is shorter than its diff:
```python
import jax
import jax.numpy as jnp
from jax import lax
from jax.sharding import PartitionSpec as P

STEPS = 2
AXES = ("cls", "row")

learn_rate = 2.0


def gather_rows(block):
    group = lax.axis_size("row")
    mine = lax.axis_index("row")
    height = block.shape[0]
    whole = jnp.zeros((height * group, block.shape[1]), block.dtype)
    whole = lax.dynamic_update_slice(whole, block, (mine * height, 0))
    paired = group & (group - 1) == 0
    for k in range(1, group):
        if paired:
            source = mine ^ k
            hops = [(i, i ^ k) for i in range(group)]
        else:
            source = (mine - k) % group
            hops = [(i, (i + k) % group) for i in range(group)]
        whole = lax.dynamic_update_slice(
            whole, lax.ppermute(block, "row", hops), (source * height, 0)
        )
    return whole


def exchange(logits, label_hit):
    peers = lax.axis_size(AXES)
    peak = jnp.max(logits, axis=1)
    mass = peak + jnp.log(jnp.sum(jnp.exp(logits - peak[:, None]), axis=1))
    picked = jnp.sum(jnp.where(label_hit, logits, 0.0), axis=1)
    packed = jnp.concatenate([mass.reshape(-1, 128), picked.reshape(-1, 128)])
    sent = jnp.broadcast_to(packed[None], (peers, *packed.shape))
    got = lax.all_to_all(sent, AXES, 0, 0, tiled=True)
    half = packed.shape[0] // 2
    masses = got[:, :half]
    top = jnp.max(masses, axis=0)
    log_norm = top + jnp.log(jnp.sum(jnp.exp(masses - top), axis=0))
    picked = jnp.sum(got[:, half:], axis=0)
    return log_norm.reshape(-1), picked.reshape(-1)


def shards(embeddings, weights, labels):
    peers = lax.axis_size(AXES)
    feature_rows = weights.shape[0]
    class_count = weights.shape[1] // peers
    examples = gather_rows(embeddings.astype(jnp.bfloat16))
    row_count = examples.shape[0]
    rate = learn_rate / row_count
    pieces = weights.astype(jnp.bfloat16).reshape(feature_rows, peers, class_count)
    block = lax.all_to_all(pieces.transpose(1, 0, 2), AXES, 0, 0, tiled=True)
    block = block.reshape(feature_rows * peers, class_count)
    gram = lax.dot_general(
        examples, examples, (((1,), (1,)), ((), ())), preferred_element_type=jnp.float32
    )
    gram = (gram * rate).astype(jnp.bfloat16)
    offset = lax.axis_index(AXES) * class_count
    columns = lax.broadcasted_iota(jnp.int32, (1, class_count), 1) + offset
    label_hit = columns == labels[:, None]
    onehot = jnp.where(label_hit, 1.0, 0.0)
    logits = jnp.dot(examples, block, preferred_element_type=jnp.float32)
    loss_rows = []
    total = 0.0
    for step_index in range(STEPS):
        if step_index > 0:
            logits = logits - jnp.dot(gram, residual, preferred_element_type=jnp.float32)
        log_norm, picked = exchange(logits, label_hit)
        loss_rows.append(log_norm - picked)
        residual = jnp.exp(logits - log_norm[:, None]) - onehot
        total = total + residual
        residual = residual.astype(jnp.bfloat16)
    update = lax.dot_general(
        examples,
        total.astype(jnp.bfloat16),
        (((0,), (0,)), ((), ())),
        preferred_element_type=jnp.float32,
    )
    return (update * -rate, jnp.stack(loss_rows))


def solution(mesh):
    placed = (P("row", None), P(AXES, None), P())
    return jax.shard_map(
        shards,
        mesh=mesh,
        in_specs=placed,
        out_specs=(P(None, AXES), P()),
        check_vma=False,
    )
```

time: 575 us -> 217 us (0.38); the launches traced: 569 us -> 217 us
  blocking collectives: 158 us -> 26.8 us
  waiting for transfers between devices: 235 us -> 112 us
  local copies, waits for them, and re-layouts: 87.6 us -> 12.3 us
  between operations: 14.6 us -> 0.79 us
  matrix products: 52.9 us -> 39.5 us
    all_to_all x1, waiting for transfers between devices: 235 us -> 41.6 us  [shards(): block = lax.all_to_all(pieces.transpose(1, 0, 2), AXES, 0, 0, tiled=True)]
    psum x2 -> x0, blocking collectives: 81.7 us -> none  [shards(): lax.psum((jnp.sum(jnp.exp(logits - row_peak[:, None]), axis=1), local_pic...]
    pmax x2 -> x0, blocking collectives: 76.5 us -> none  [shards(): row_peak = lax.pmax(local_peak, ('cls', 'row'))]
    ppermute x0 -> x3, waiting for transfers between devices: none -> 70.7 us  [gather_rows(): lax.ppermute(block, 'row', hops)]
    all_to_all x0 -> x2, blocking collectives: none -> 26.8 us  [exchange(): got = lax.all_to_all(sent, AXES, 0, 0, tiled=True)]
    reshape x2 -> x0, local copies, waits for them, and re-layouts: 24.2 us -> none  [shards(): pieces = weights.reshape(feature_rows, peer_count, class_count // 128, 128)]
    all_to_all x1 -> x0, local copies, waits for them, and re-layouts: 17.8 us -> none  [shards(): lax.all_to_all(pieces, ('cls', 'row'), split_axis=1, concat_axis=0, tiled...]
    unnamed x14 -> x9, local copies, waits for them, and re-layouts: 22.8 us -> 5.61 us
  transfers between devices with their start and end apart: 2 -> 4, of which waited for: 1 -> 4; matrix products, arithmetic and copies ran while one was open for 7% -> 1% of each run, Pallas kernels for 0% -> 0%
where the time goes in v1:
time: 217 us
  waiting for transfers between devices  112 us (52%)
  matrix products  39.5 us (18%)
  blocking collectives  26.8 us (12%)
  other arithmetic  15.7 us (7%)
  local copies, waits for them, and re-layouts  12.3 us (6%)
  starting transfers between devices  9.3 us (4%)
    ppermute x3, waiting for transfers between devices, gather_rows(): lax.ppermute(block, 'row', hops)  70.7 us
    all_to_all x1, waiting for transfers between devices, shards(): block = lax.all_to_all(pieces.transpose(1, 0, 2), AXES, 0, 0, tiled=True)  41.6 us
    all_to_all x2, blocking collectives, exchange(): got = lax.all_to_all(sent, AXES, 0, 0, tiled=True)  26.8 us
    dot_general x1, matrix products, shards(): jnp.dot(gram, residual, preferred_element_type=jnp.float32)  19.1 us
    dot_general x1, matrix products, shards(): lax.dot_general(examples, total.astype(jnp.bfloat16), (((0,), (0,)), ((),...  12.7 us
    reduce_sum x2, other arithmetic, exchange(): mass = peak + jnp.log(jnp.sum(jnp.exp(logits - peak[:, None]), axis=1))  9.42 us
    dot_general x1, matrix products, shards(): logits = jnp.dot(examples, block, preferred_element_type=jnp.float32)  7.68 us
    all_to_all x1, starting transfers between devices, shards(): block = lax.all_to_all(pieces.transpose(1, 0, 2), AXES, 0, 0, tiled=True)  7.44 us
  transfers between devices with their start and end apart: 4, of which 4 were waited for; matrix products, arithmetic and copies ran while one was open for 1% of the time, Pallas kernels for 0%

profile of v1, /device:TPU:0, one launch (start us, length us, event | category | flops | bytes accessed | tf_op | source)
XLA Modules:
  0.0 216.7 jit_solution(12905247446465332294)
XLA Ops:
  0.6 4.5 %convert_element_type.16 = bf16[32,81920]{1,0:T(8,128)(2,1)S(1)} convert(f32[32,81920]{1,0:T(8,128)} %param.4) | non-fusion elementwise | flops 2621440 | bytes 15728640 | tf_op jit(solution)/shard_map/convert_element_type | solution.py:55
  5.1 1.6 copy.8
  6.7 0.0 copy-start.2
  6.8 5.2 %copy.7 = bf16[32,32,2560]{2,1,0:T(8,128)(2,1)} copy(bf16[32,32,2560]{2,0,1:T(8,128)(2,1)S(1)} %bitcast.22) | data formatting | bytes 10485760 | tf_op jit(solution)/shard_map/transpose | solution.py:56
  12.0 7.4 %all-to-all-start = ((bf16[32,32,2560]{2,1,0:T(8,128)(2,1)}), bf16[32,32,2560]{2,1,0:T(8,128)(2,1)}, u32[]{:S(2)}, u32[]{:S(2)}) async-start(bf16[32,32,2560]{2,1,0:T(8,128)(2,1)} %copy.7), calls=%async_computation | async-start | bytes 10485760 | tf_op jit(solution)/shard_map/all_to_all | solution.py:56
  19.4 0.3 broadcast_in_dim.17
  19.7 0.0 copy-done.2
  19.7 1.0 constant_dynamic-update-slice_fusion.3
  20.7 0.2 collective-permute-start
  20.9 1.6 collective-permute-start.1
  22.5 0.0 collective-permute-start.2
  22.5 0.4 collective-permute-done
  22.9 1.1 constant_dynamic-update-slice_fusion.2
  24.0 55.2 %collective-permute-done.1 = bf16[256,1024]{1,0:T(8,128)(2,1)S(1)} collective-permute-done((bf16[256,1024]{1,0:T(8,128)(2,1)}, bf16[256,1024]{1,0:T(8,128)(2,1)S(1)}, u32[]{:S(2)}, u32[]{:S(2)}) %collective-permute-start.1) | collective-permute-done | bytes 524320 | tf_op jit(solution)/shard_map/ppermute | solution.py:27
  79.3 15.0 %collective-permute-done.2 = bf16[256,1024]{1,0:T(8,128)(2,1)S(1)} collective-permute-done((bf16[256,1024]{1,0:T(8,128)(2,1)}, bf16[256,1024]{1,0:T(8,128)(2,1)S(1)}, u32[]{:S(2)}, u32[]{:S(2)}) %collective-permute-start.2) | collective-permute-done | bytes 524320 | tf_op jit(solution)/shard_map/ppermute | solution.py:27
  94.4 41.6 %all-to-all-done = bf16[32,32,2560]{2,1,0:T(8,128)(2,1)} async-done(((bf16[32,32,2560]{2,1,0:T(8,128)(2,1)}), bf16[32,32,2560]{2,1,0:T(8,128)(2,1)}, u32[]{:S(2)}, u32[]{:S(2)}) %all-to-all-start) | async-done | bytes 5242912 | tf_op jit(solution)/shard_map/all_to_all | solution.py:56
  136.0 0.0 copy-start.3
  136.0 7.7 %fusion.23 = (f32[1024]{0:T(1024)S(1)}, f32[1024,2560]{1,0:T(8,128)S(1)}) fusion(bf16[1024,1024]{1,0:T(8,128)(2,1)S(1)} %constant_dynamic-update-slice_fusion, bf16[1024,2560]{1,0:T(8,128)(2,1)} %bitcast.1), kind=kOutput, calls=%fused_computation.47 | convolution fusion | flops 5371329536 | bytes 17829888 | tf_op jit(solution)/shard_map/dot_general | solution.py:66
  143.7 0.0 copy-start
  143.7 4.0 %copy-done = f32[1024,2560]{1,0:T(8,128)} copy-done((f32[1024,2560]{1,0:T(8,128)}, f32[1024,2560]{1,0:T(8,128)S(1)}, u32[]{:S(2)}) %copy-start) | copy-done | bytes 10485784
  147.7 0.0 copy-done.3
  147.7 3.1 %exponential_reduce_fusion.1 = (f32[1024]{0:T(1024)S(1)}, f32[1024]{0:T(1024)S(1)}) fusion(f32[1024,2560]{1,0:T(8,128)S(1)} %get-tuple-element.17, f32[1024]{0:T(1024)S(1)} %get-tuple-element.16, s32[1024]{0:T(1024)S(1)} %copy-done.3, s32[2560]{0:T(1024)S(1)} %iota_add_fusion), kind=kLoop, calls=%fused_computation.10 | loop fusion | flops 13105152 | bytes 10512384 | tf_op jit(solution)/shard_map/reduce_sum | solution.py:35
  150.8 14.0 %all_to_all.15 = f32[32,16,128]{2,1,0:T(8,128)S(1)} all-to-all(f32[32,16,128]{2,1,0:T(8,128)S(1)} %broadcast_in_dim.19), channel_id=1, replica_groups=mesh['cls'=8,'row'=4] {'cls','row'}, dimensions={0} | all-to-all | bytes 524288 | tf_op jit(solution)/shard_map/all_to_all | solution.py:39
  165.0 19.1 %fusion.24 = (f32[1024]{0:T(1024)S(1)}, f32[1024,2560]{1,0:T(8,128)}) fusion(f32[1024,2560]{1,0:T(8,128)} %copy-done, f32[1024]{0:T(1024)S(1)} %get-tuple-element.13, s32[2560]{0:T(1024)S(1)} %iota_add_fusion, s32[1024]{0:T(1024)S(1)} %copy-done.3, bf16[1024,1024]{1,0:T(8,128)(2,1)S(1)} %constant_dynamic-update-slice_fusion), kind=kOutput, calls=%fused_computation.48 | convolution fusion | flops 7536638976 | bytes 23091200 | tf_op jit(solution)/shard_map/dot_general | solution.py:71
  184.1 0.0 copy-start.1
  184.1 6.4 %exponential_reduce_fusion = (f32[1024]{0:T(1024)S(1)}, f32[1024]{0:T(1024)S(1)}) fusion(f32[1024,2560]{1,0:T(8,128)} %get-tuple-element.19, f32[1024]{0:T(1024)S(1)} %get-tuple-element.18, s32[1024]{0:T(1024)S(1)} %copy-done.3, s32[2560]{0:T(1024)S(1)} %iota_add_fusion), kind=kLoop, calls=%fused_computation.9 | loop fusion | flops 13105152 | bytes 10512384 | tf_op jit(solution)/shard_map/reduce_sum | solution.py:35
  190.5 12.8 %all_to_all.16 = f32[32,16,128]{2,1,0:T(8,128)S(1)} all-to-all(f32[32,16,128]{2,1,0:T(8,128)S(1)} %broadcast_in_dim.35), channel_id=1, replica_groups=mesh['cls'=8,'row'=4] {'cls','row'}, dimensions={0} | all-to-all | bytes 524288 | tf_op jit(solution)/shard_map/all_to_all | solution.py:39
  203.4 0.0 copy-done.1
  203.4 12.7 %convolution_multiply_fusion = f32[1024,2560]{1,0:T(8,128)} fusion(bf16[1024,1024]{1,0:T(8,128)(2,1)S(1)} %constant_dynamic-update-slice_fusion, f32[1024,2560]{1,0:T(8,128)S(1)} %copy-done.1, f32[1024,2560]{1,0:T(8,128)} %copy-done, f32[1024]{0:T(1024)S(1)} %get-tuple-element.15, f32[1024]{0:T(1024)S(1)} %get-tuple-element.13, s32[2560]{0:T(1024)S(1)} %iota_add_fusion, ...), kind=kOutput, calls=%fused_computation.12 | convolution fusion | flops 5392302080 | bytes 33576960 | tf_op jit(solution)/shard_map/dot_general | solution.py:77
  216.1 0.6 pad_maximum_fusion.2
  (15 shorter events, 0.3 us)
Async XLA Ops:
  6.7 13.0 %copy-start.2 = (f32[256,1024]{1,0:T(8,128)S(1)}, f32[256,1024]{1,0:T(8,128)}, u32[]{:S(2)}) copy-start(f32[256,1024]{1,0:T(8,128)} %param.3) | copy-start | bytes 3145732
  12.0 124.0 %all-to-all-start = ((bf16[32,32,2560]{2,1,0:T(8,128)(2,1)}), bf16[32,32,2560]{2,1,0:T(8,128)(2,1)}, u32[]{:S(2)}, u32[]{:S(2)}) async-start(bf16[32,32,2560]{2,1,0:T(8,128)(2,1)} %copy.7), calls=%async_computation | async-start | bytes 10485760 | tf_op jit(solution)/shard_map/all_to_all | solution.py:56
  20.7 2.3 %collective-permute-start = (bf16[256,1024]{1,0:T(8,128)(2,1)}, bf16[256,1024]{1,0:T(8,128)(2,1)}, u32[]{:S(2)}, u32[]{:S(2)}) collective-permute-start(bf16[256,1024]{1,0:T(8,128)(2,1)} %get-tuple-element.11), channel_id=1, source_target_pairs={{0,1},{1,0},{2,3},{3,2},{4,5},{5,4},{6,7},{7,6},{8,9},{9,8},{10,11... | collective-permute-start | bytes 1572872 | tf_op jit(solution)/shard_map/ppermute | solution.py:27
  20.9 58.4 %collective-permute-start.1 = (bf16[256,1024]{1,0:T(8,128)(2,1)}, bf16[256,1024]{1,0:T(8,128)(2,1)S(1)}, u32[]{:S(2)}, u32[]{:S(2)}) collective-permute-start(bf16[256,1024]{1,0:T(8,128)(2,1)} %get-tuple-element.11), channel_id=1, source_target_pairs={{0,2},{1,3},{2,0},{3,1},{4,6},{5,7},{6,4},{7,5},{8,10},{9,11},{10,... | collective-permute-start | bytes 1572872 | tf_op jit(solution)/shard_map/ppermute | solution.py:27
  22.5 71.8 %collective-permute-start.2 = (bf16[256,1024]{1,0:T(8,128)(2,1)}, bf16[256,1024]{1,0:T(8,128)(2,1)S(1)}, u32[]{:S(2)}, u32[]{:S(2)}) collective-permute-start(bf16[256,1024]{1,0:T(8,128)(2,1)} %get-tuple-element.11), channel_id=1, source_target_pairs={{0,3},{1,2},{2,1},{3,0},{4,7},{5,6},{6,5},{7,4},{8,11},{9,10},{10,... | collective-permute-start | bytes 1572872 | tf_op jit(solution)/shard_map/ppermute | solution.py:27
  136.0 11.7 %copy-start.3 = (s32[1024]{0:T(1024)S(1)}, s32[1024]{0:T(1024)}, u32[]{:S(2)}) copy-start(s32[1024]{0:T(1024)} %param.5) | copy-start | bytes 12292
  143.7 4.0 %copy-start = (f32[1024,2560]{1,0:T(8,128)}, f32[1024,2560]{1,0:T(8,128)S(1)}, u32[]{:S(2)}) copy-start(f32[1024,2560]{1,0:T(8,128)S(1)} %get-tuple-element.17) | copy-start | bytes 31457284
  184.1 19.3 %copy-start.1 = (f32[1024,2560]{1,0:T(8,128)S(1)}, f32[1024,2560]{1,0:T(8,128)}, u32[]{:S(2)}) copy-start(f32[1024,2560]{1,0:T(8,128)} %get-tuple-element.19) | copy-start | bytes 31457284

commit v2 on v1

v2 whole, which is shorter than its diff:
```python
import functools

import jax
import jax.numpy as jnp
from jax import lax
from jax.experimental import pallas as pl
from jax.experimental.pallas import tpu as pltpu
from jax.sharding import PartitionSpec as P

AXES = ("cls", "row")
LANES = 128
MIB = 1 << 20

learn_rate = 2.0

WHOLE = pl.BlockSpec(memory_space=pltpu.VMEM)


def tile(width):
    return next(t for t in (512, 256, 128) if width % t == 0)


def diagonal():
    rows = lax.broadcasted_iota(jnp.int32, (LANES, LANES), 0)
    lanes = lax.broadcasted_iota(jnp.int32, (LANES, LANES), 1)
    return rows == lanes


def to_row(column):
    keep = diagonal()
    parts = []
    for start in range(0, column.shape[0], LANES):
        spread = jnp.broadcast_to(column[start : start + LANES], (LANES, LANES))
        parts.append(jnp.sum(jnp.where(keep, spread, 0.0), axis=0, keepdims=True))
    return jnp.concatenate(parts, axis=1)


def to_column(row):
    keep = diagonal()
    parts = []
    for start in range(0, row.shape[1], LANES):
        spread = jnp.broadcast_to(row[:, start : start + LANES], (LANES, LANES))
        parts.append(jnp.sum(jnp.where(keep, spread, 0.0), axis=1, keepdims=True))
    return jnp.concatenate(parts, axis=0)


def combine(got):
    masses = got[:, 0:1, :]
    top = jnp.max(masses, axis=0)
    log_norm = top + jnp.log(jnp.sum(jnp.exp(masses - top[None]), axis=0))
    return log_norm, jnp.sum(got[:, 1:2, :], axis=0)


def tally(logits, hits, first, peak_ref, mass_ref, pick_ref):
    groups = [logits[:, g : g + LANES] for g in range(0, logits.shape[1], LANES)]
    peak = functools.reduce(jnp.maximum, groups)
    if not first:
        peak = jnp.maximum(peak, peak_ref[...])
    mass = sum(jnp.exp(g - peak) for g in groups)
    pick = sum(jnp.where(h, g, 0.0) for g, h in zip(groups, hits))
    if not first:
        mass = mass + mass_ref[...] * jnp.exp(peak_ref[...] - peak)
        pick = pick + pick_ref[...]
    peak_ref[...] = peak
    mass_ref[...] = mass
    pick_ref[...] = pick


def finish(out_ref, peak_ref, mass_ref, pick_ref):
    lanes_peak = peak_ref[...]
    peak = jnp.max(lanes_peak, axis=1, keepdims=True)
    mass = jnp.sum(mass_ref[...] * jnp.exp(lanes_peak - peak), axis=1, keepdims=True)
    pick = jnp.sum(pick_ref[...], axis=1, keepdims=True)
    rows = jnp.concatenate([to_row(peak + jnp.log(mass)), to_row(pick)], axis=0)
    out_ref[...] = jnp.broadcast_to(rows[None], out_ref.shape)


def hits_of(places, start, width):
    lane = lax.broadcasted_iota(jnp.int32, (1, LANES), 1)
    return [places == lane + (start + g) for g in range(0, width, LANES)]


def cast_kernel(in_ref, out_ref):
    width = out_ref.shape[2]
    for k in range(out_ref.shape[0]):
        out_ref[k] = in_ref[:, k * width : (k + 1) * width].astype(out_ref.dtype)


def first_kernel(places_ref, x_ref, w_ref, logits_ref, sent_ref, peak_ref, mass_ref, pick_ref):
    width = w_ref.shape[1]
    step = tile(width)
    places = places_ref[...]
    for start in range(0, width, step):
        block = slice(start, start + step)
        logits = jnp.dot(x_ref[...], w_ref[:, block], preferred_element_type=jnp.float32)
        logits_ref[:, block] = logits
        tally(logits, hits_of(places, start, step), start == 0, peak_ref, mass_ref, pick_ref)
    finish(sent_ref, peak_ref, mass_ref, pick_ref)


def second_kernel(
    got_ref, places_ref, gram_ref, old_ref,
    residual_ref, logits_ref, sent_ref, peak_ref, mass_ref, pick_ref,
):
    width = old_ref.shape[1]
    step = tile(width)
    log_norm, _ = combine(got_ref[...])
    norm = to_column(log_norm)
    places = places_ref[...]
    for start in range(0, width, step):
        block = slice(start, start + step)
        hits = hits_of(places, start, step)
        old = old_ref[:, block]
        chance = jnp.exp(old - norm)
        onehot = jnp.concatenate([jnp.where(h, 1.0, 0.0) for h in hits], axis=1)
        residual = (chance - onehot).astype(jnp.bfloat16)
        residual_ref[:, block] = residual
        logits = old - jnp.dot(gram_ref[...], residual, preferred_element_type=jnp.float32)
        logits_ref[:, block] = logits
        tally(logits, hits, start == 0, peak_ref, mass_ref, pick_ref)
    finish(sent_ref, peak_ref, mass_ref, pick_ref)


def last_kernel(
    rate, before_ref, got_ref, places_ref, flipped_ref, residual_ref, logits_ref,
    update_ref, losses_ref, buffer_ref, sems,
):
    width = logits_ref.shape[1]
    step = tile(width)
    old_norm, old_pick = combine(before_ref[...])
    log_norm, pick = combine(got_ref[...])
    losses_ref[...] = jnp.concatenate([old_norm - old_pick, log_norm - pick], axis=0)
    norm = to_column(log_norm)
    places = places_ref[...]

    def copy(start):
        slot = start // step % 2
        return pltpu.make_async_copy(
            buffer_ref.at[slot], update_ref.at[:, pl.ds(start, step)], sems.at[slot]
        )

    for start in range(0, width, step):
        block = slice(start, start + step)
        hits = hits_of(places, start, step)
        chance = jnp.exp(logits_ref[:, block] - norm)
        onehot = jnp.concatenate([jnp.where(h, 1.0, 0.0) for h in hits], axis=1)
        total = residual_ref[:, block].astype(jnp.float32) + (chance - onehot)
        update = jnp.dot(
            flipped_ref[...], total.astype(jnp.bfloat16), preferred_element_type=jnp.float32
        )
        if start >= 2 * step:
            copy(start - 2 * step).wait()
        buffer_ref[start // step % 2] = update * -rate
        copy(start).start()
    for start in range(max(0, width - 2 * step), width, step):
        copy(start).wait()


def grant(mib):
    return pltpu.CompilerParams(vmem_limit_bytes=mib * MIB)


def gather_rows(block):
    group = lax.axis_size("row")
    mine = lax.axis_index("row")
    height = block.shape[0]
    whole = jnp.zeros((height * group, block.shape[1]), block.dtype)
    whole = lax.dynamic_update_slice(whole, block, (mine * height, 0))
    paired = group & (group - 1) == 0
    for k in range(1, group):
        if paired:
            source = mine ^ k
            hops = [(i, i ^ k) for i in range(group)]
        else:
            source = (mine - k) % group
            hops = [(i, (i + k) % group) for i in range(group)]
        whole = lax.dynamic_update_slice(
            whole, lax.ppermute(block, "row", hops), (source * height, 0)
        )
    return whole


def trade(sent):
    return lax.all_to_all(sent, AXES, 0, 0, tiled=True)


def shards(embeddings, weights, labels):
    peers = lax.axis_size(AXES)
    depth = weights.shape[0]
    classes = weights.shape[1] // peers
    f32, bf16 = jnp.float32, jnp.bfloat16
    chunk = 4 if peers % 4 == 0 else 1
    pieces = pl.pallas_call(
        cast_kernel,
        grid=(peers // chunk,),
        in_specs=[pl.BlockSpec((depth, chunk * classes), lambda i: (0, i))],
        out_specs=pl.BlockSpec((chunk, depth, classes), lambda i: (i, 0, 0)),
        out_shape=jax.ShapeDtypeStruct((peers, depth, classes), bf16),
    )(weights)
    block = lax.all_to_all(pieces, AXES, 0, 0, tiled=True)
    block = block.reshape(depth * peers, classes)

    examples = gather_rows(embeddings.astype(bf16))
    rows = examples.shape[0]
    rate = learn_rate / rows
    gram = lax.dot_general(examples, examples, (((1,), (1,)), ((), ())), preferred_element_type=f32)
    gram = (gram * rate).astype(bf16)
    flipped = examples.T
    places = labels - lax.axis_index(AXES) * classes
    places = jnp.broadcast_to(places[:, None], (rows, LANES))

    logits_shape = pltpu.VMEM((rows, classes), f32)
    stats_shape = jax.ShapeDtypeStruct((peers, 2, rows), f32)
    scratch = [pltpu.VMEM((rows, LANES), f32)] * 3
    logits, sent = pl.pallas_call(
        first_kernel,
        in_specs=[WHOLE] * 3,
        out_specs=[WHOLE] * 2,
        out_shape=[logits_shape, stats_shape],
        scratch_shapes=scratch,
        compiler_params=grant(16),
    )(places, examples, block)
    before = trade(sent)
    residual, logits, sent = pl.pallas_call(
        second_kernel,
        in_specs=[WHOLE] * 4,
        out_specs=[WHOLE] * 3,
        out_shape=[pltpu.VMEM((rows, classes), bf16), logits_shape, stats_shape],
        scratch_shapes=scratch,
        compiler_params=grant(16),
    )(before, places, gram, logits)
    got = trade(sent)
    step = tile(classes)
    update, losses = pl.pallas_call(
        functools.partial(last_kernel, rate),
        in_specs=[WHOLE] * 6,
        out_specs=[pl.BlockSpec(memory_space=pltpu.HBM), WHOLE],
        out_shape=[
            jax.ShapeDtypeStruct((depth * peers, classes), f32),
            jax.ShapeDtypeStruct((2, rows), f32),
        ],
        scratch_shapes=[pltpu.VMEM((2, depth * peers, step), f32), pltpu.SemaphoreType.DMA((2,))],
        compiler_params=grant(16),
    )(before, got, places, flipped, residual, logits)
    return update, losses


def solution(mesh):
    placed = (P("row", None), P(AXES, None), P())
    return jax.shard_map(
        shards,
        mesh=mesh,
        in_specs=placed,
        out_specs=(P(None, AXES), P()),
        check_vma=False,
    )
```

time: 217 us -> 202 us (0.931)
  Pallas kernels: 0 us -> 37.6 us
  matrix products: 39.5 us -> 3.73 us
  other arithmetic: 15.7 us -> 0.01 us
  blocking collectives: 26.8 us -> 12.8 us
  local copies, waits for them, and re-layouts: 12.3 us -> 16.8 us
  waiting for transfers between devices: 112 us -> 116 us
  starting transfers between devices: 9.3 us -> 13.2 us
    pallas_call x0 -> x4, Pallas kernels: none -> 37.6 us  [the longest x1 10 us: shards(): pl.pallas_call(functools.partial(last_kernel, rate), in_specs=[WHOLE] * 6...]
    dot_general x3 -> x1, matrix products: 39.5 us -> 3.73 us  [shards(): lax.dot_general(examples, examples, (((1,), (1,)), ((), ())), preferred_e...]
    all_to_all x2 -> x1, blocking collectives: 26.8 us -> 12.8 us  [trade(): return lax.all_to_all(sent, AXES, 0, 0, tiled=True)]
    reduce_sum x4 -> x0, other arithmetic: 9.51 us -> none  [the longest x2 9.42 us: exchange(): mass = peak + jnp.log(jnp.sum(jnp.exp(logits - peak[:, None]), axis=1))]
    unnamed x9 -> x13, local copies, waits for them, and re-layouts: 5.61 us -> 11.5 us
    transpose x1 -> x0, local copies, waits for them, and re-layouts: 5.23 us -> none  [shards(): block = lax.all_to_all(pieces.transpose(1, 0, 2), AXES, 0, 0, tiled=True)]
    convert_element_type x1 -> x0, other arithmetic: 4.49 us -> none  [shards(): weights.astype(jnp.bfloat16).reshape(feature_rows, peers, class_count)]
    all_to_all x1 -> x2, waiting for transfers between devices: 41.6 us -> 45.7 us  [the longest x1 39 us: shards(): block = lax.all_to_all(pieces, AXES, 0, 0, tiled=True)]
  transfers between devices with their start and end apart: 4 -> 5, of which waited for: 4 -> 4; matrix products, arithmetic and copies ran while one was open for 1% -> 5% of each run, Pallas kernels for 0% -> 0%
where the time goes in v2:
time: 202 us; the launch traced here: 201 us
  waiting for transfers between devices  116 us (57%)
  Pallas kernels  37.6 us (19%)
  local copies, waits for them, and re-layouts  16.8 us (8%)
  starting transfers between devices  13.2 us (7%)
  blocking collectives  12.8 us (6%)
  matrix products  3.73 us (2%)
    ppermute x3, waiting for transfers between devices, gather_rows(): lax.ppermute(block, 'row', hops)  70.1 us
    all_to_all x1, waiting for transfers between devices, shards(): block = lax.all_to_all(pieces, AXES, 0, 0, tiled=True)  39 us
    all_to_all x1, blocking collectives, trade(): return lax.all_to_all(sent, AXES, 0, 0, tiled=True)  12.8 us
    unnamed x13, local copies, waits for them, and re-layouts  11.5 us
    pallas_call x1, Pallas kernels, shards(): pl.pallas_call(functools.partial(last_kernel, rate), in_specs=[WHOLE] * 6...  10 us
    pallas_call x1, Pallas kernels, shards(): pl.pallas_call(first_kernel, in_specs=[WHOLE] * 3, out_specs=[WHOLE] * 2,...  9.71 us
    pallas_call x1, Pallas kernels, shards(): pl.pallas_call(second_kernel, in_specs=[WHOLE] * 4, out_specs=[WHOLE] * 3...  9.48 us
    pallas_call x1, Pallas kernels, shards(): pl.pallas_call(cast_kernel, grid=(peers // chunk,), in_specs=[pl.BlockSpe...  8.43 us
  transfers between devices with their start and end apart: 5, of which 4 were waited for; matrix products, arithmetic and copies ran while one was open for 5% of the time, Pallas kernels for 0%

profile of v2, /device:TPU:0, one launch (start us, length us, event | category | flops | bytes accessed | tf_op | source)
XLA Modules:
  0.0 201.0 jit_solution(2026700560039079538)
XLA Ops:
  0.6 8.4 %shard_map.50 = bf16[32,32,2560]{2,1,0:T(8,128)(2,1)} custom-call(f32[32,81920]{1,0:T(8,128)} %in_ref.1), custom_call_target="tpu_custom_call" | custom-call | tf_op jit(solution)/shard_map/pallas_call | solution.py:193
  9.1 0.0 copy-start.4
  9.1 7.4 %all-to-all-start = ((bf16[32,32,2560]{2,1,0:T(8,128)(2,1)}), bf16[32,32,2560]{2,1,0:T(8,128)(2,1)}, u32[]{:S(2)}, u32[]{:S(2)}) async-start(bf16[32,32,2560]{2,1,0:T(8,128)(2,1)} %shard_map.50), calls=%async_computation | async-start | bytes 10485760 | tf_op jit(solution)/shard_map/all_to_all | solution.py:200
  16.5 0.0 copy-done.4
  16.5 0.0 copy-start.5
  16.5 0.2 copy.5
  16.7 0.3 collective-permute-start
  17.0 1.6 collective-permute-start.1
  18.6 0.0 collective-permute-start.2
  18.7 0.3 broadcast_in_dim.10
  18.9 0.1 constant_dynamic-update-slice_fusion.3
  19.0 0.0 copy-done.5
  19.1 0.0 collective-permute-done
  19.1 1.1 constant_dynamic-update-slice_fusion.2
  20.2 56.2 %collective-permute-done.1 = bf16[256,1024]{0,1:T(8,128)(2,1)} collective-permute-done((bf16[256,1024]{0,1:T(8,128)(2,1)S(1)}, bf16[256,1024]{0,1:T(8,128)(2,1)}, u32[]{:S(2)}, u32[]{:S(2)}) %collective-permute-start.1) | collective-permute-done | bytes 524320 | tf_op jit(solution)/shard_map/ppermute | solution.py:178
  76.4 1.1 constant_dynamic-update-slice_fusion.1
  77.5 13.9 %collective-permute-done.2 = bf16[256,1024]{0,1:T(8,128)(2,1)S(1)} collective-permute-done((bf16[256,1024]{0,1:T(8,128)(2,1)S(1)}, bf16[256,1024]{0,1:T(8,128)(2,1)S(1)}, u32[]{:S(2)}, u32[]{:S(2)}) %collective-permute-start.2) | collective-permute-done | bytes 524320 | tf_op jit(solution)/shard_map/ppermute | solution.py:178
  91.4 0.1 constant_dynamic-update-slice_fusion
  91.5 2.6 %copy.6.x_ref = bf16[1024,1024]{1,0:T(8,128)(2,1)} copy(bf16[1024,1024]{0,1:T(8,128)(2,1)S(1)} %constant_dynamic-update-slice_fusion) | data formatting | bytes 4194304 | tf_op jit(solution)/shard_map/dynamic_update_slice | solution.py:177
  94.1 39.0 %all-to-all-done = bf16[32,32,2560]{2,1,0:T(8,128)(2,1)} async-done(((bf16[32,32,2560]{2,1,0:T(8,128)(2,1)}), bf16[32,32,2560]{2,1,0:T(8,128)(2,1)}, u32[]{:S(2)}, u32[]{:S(2)}) %all-to-all-start) | async-done | bytes 5242912 | tf_op jit(solution)/shard_map/all_to_all | solution.py:200
  133.1 0.2 broadcast_in_dim.4.places_ref
  133.3 0.0 copy-start.2
  133.3 1.6 copy-done.2
  134.9 9.7 %shard_map.51 = (f32[1024,2560]{1,0:T(8,128)S(1)}, f32[32,2,1024]{2,1,0:T(2,128)}) custom-call(s32[1024,128]{1,0:T(8,128)S(1)} %broadcast_in_dim.4.places_ref, bf16[1024,1024]{1,0:T(8,128)(2,1)S(1)} %copy-done.2, bf16[1024,2560]{1,0:T(8,128)(2,1)} %bitcast.w_ref), custom_call_target="tpu_custom_call" | custom-call | tf_op jit(solution)/shard_map/pallas_call | solution.py:215
  144.6 0.0 copy-start
  144.6 4.1 %copy-done = f32[1024,2560]{1,0:T(8,128)} copy-done((f32[1024,2560]{1,0:T(8,128)}, f32[1024,2560]{1,0:T(8,128)S(1)}, u32[]{:S(2)}) %copy-start) | copy-done | bytes 10485784
  148.7 3.8 %all-to-all-start.1 = ((f32[32,2,1024]{2,1,0:T(2,128)}), f32[32,2,1024]{2,1,0:T(2,128)S(1)}, u32[]{:S(2)}, u32[]{:S(2)}) async-start(f32[32,2,1024]{2,1,0:T(2,128)} %get-tuple-element.7), calls=%async_computation.1 | async-start | bytes 524288 | tf_op jit(solution)/shard_map/all_to_all | solution.py:184
  152.5 3.7 %multiply_convert_fusion.gram_ref = bf16[1024,1024]{1,0:T(8,128)(2,1)} fusion(bf16[1024,1024]{0,1:T(8,128)(2,1)S(1)} %constant_dynamic-update-slice_fusion), kind=kOutput, calls=%fused_computation | convolution fusion | flops 2149580800 | bytes 4194304 | tf_op jit(solution)/shard_map/dot_general | solution.py:206
  156.3 6.7 %all-to-all-done.1.got_ref.before_ref = f32[32,2,1024]{2,1,0:T(2,128)S(1)} async-done(((f32[32,2,1024]{2,1,0:T(2,128)}), f32[32,2,1024]{2,1,0:T(2,128)S(1)}, u32[]{:S(2)}, u32[]{:S(2)}) %all-to-all-start.1) | async-done | bytes 262176 | tf_op jit(solution)/shard_map/all_to_all | solution.py:184
  162.9 0.0 copy-start.1
  162.9 4.0 %copy-done.1 = f32[1024,2560]{1,0:T(8,128)S(1)} copy-done((f32[1024,2560]{1,0:T(8,128)S(1)}, f32[1024,2560]{1,0:T(8,128)}, u32[]{:S(2)}) %copy-start.1) | copy-done | bytes 10485784
  166.9 0.0 copy-start.3
  166.9 1.6 copy-done.3
  168.5 9.5 %shard_map.52 = (bf16[1024,2560]{1,0:T(8,128)(2,1)S(1)}, f32[1024,2560]{1,0:T(8,128)S(1)}, f32[32,2,1024]{2,1,0:T(2,128)S(1)}) custom-call(f32[32,2,1024]{2,1,0:T(2,128)S(1)} %all-to-all-done.1.got_ref.before_ref, s32[1024,128]{1,0:T(8,128)S(1)} %broadcast_in_dim.4.places_ref, bf16[1024,1024]{1,0:T(8,128)(2,1)S(1)} %copy-done.3, f32[1024,2560]{1,0:T(8,128)S(1)} %copy-done.1), custom_call_target="tpu_custom_call" | custom-call | tf_op jit(solution)/shard_map/pallas_call | solution.py:224
  178.0 12.8 %all_to_all.15.got_ref = f32[32,2,1024]{2,1,0:T(2,128)S(1)} all-to-all(f32[32,2,1024]{2,1,0:T(2,128)S(1)} %get-tuple-element.9), channel_id=1, replica_groups=mesh['cls'=8,'row'=4] {'cls','row'}, dimensions={0} | all-to-all | bytes 524288 | tf_op jit(solution)/shard_map/all_to_all | solution.py:184
  190.8 10.0 %shard_map.53 = (f32[1024,2560]{1,0:T(8,128)}, f32[2,1024]{1,0:T(2,128)}) custom-call(f32[32,2,1024]{2,1,0:T(2,128)S(1)} %all-to-all-done.1.got_ref.before_ref, f32[32,2,1024]{2,1,0:T(2,128)S(1)} %all_to_all.15.got_ref, s32[1024,128]{1,0:T(8,128)S(1)} %broadcast_in_dim.4.places_ref, bf16[1024,1024]{1,0:T(8,128)(2,1)S(1)} %bitcast.4, ...), custom_call_target="tpu_custom_call" | custom-call | tf_op jit(solution)/shard_map/pallas_call | solution.py:234
  (1 shorter events, 0.0 us)
Async XLA Ops:
  9.1 7.5 %copy-start.4 = (f32[256,1024]{1,0:T(8,128)S(1)}, f32[256,1024]{1,0:T(8,128)}, u32[]{:S(2)}) copy-start(f32[256,1024]{1,0:T(8,128)} %param.3) | copy-start | bytes 3145732
  9.1 124.0 %all-to-all-start = ((bf16[32,32,2560]{2,1,0:T(8,128)(2,1)}), bf16[32,32,2560]{2,1,0:T(8,128)(2,1)}, u32[]{:S(2)}, u32[]{:S(2)}) async-start(bf16[32,32,2560]{2,1,0:T(8,128)(2,1)} %shard_map.50), calls=%async_computation | async-start | bytes 10485760 | tf_op jit(solution)/shard_map/all_to_all | solution.py:200
  16.5 2.5 %copy-start.5 = (s32[1024]{0:T(1024)S(1)}, s32[1024]{0:T(1024)}, u32[]{:S(2)}) copy-start(s32[1024]{0:T(1024)} %param.5) | copy-start | bytes 12292
  16.7 2.3 %collective-permute-start = (bf16[256,1024]{0,1:T(8,128)(2,1)S(1)}, bf16[256,1024]{0,1:T(8,128)(2,1)}, u32[]{:S(2)}, u32[]{:S(2)}) collective-permute-start(bf16[256,1024]{0,1:T(8,128)(2,1)S(1)} %copy.5), channel_id=1, source_target_pairs={{0,1},{1,0},{2,3},{3,2},{4,5},{5,4},{6,7},{7,6},{8,9},{9,8},{10,11... | collective-permute-start | bytes 1572872 | tf_op jit(solution)/shard_map/ppermute | solution.py:178
  17.0 59.4 %collective-permute-start.1 = (bf16[256,1024]{0,1:T(8,128)(2,1)S(1)}, bf16[256,1024]{0,1:T(8,128)(2,1)}, u32[]{:S(2)}, u32[]{:S(2)}) collective-permute-start(bf16[256,1024]{0,1:T(8,128)(2,1)S(1)} %copy.5), channel_id=1, source_target_pairs={{0,2},{1,3},{2,0},{3,1},{4,6},{5,7},{6,4},{7,5},{8,10},{9,11},{10,... | collective-permute-start | bytes 1572872 | tf_op jit(solution)/shard_map/ppermute | solution.py:178
  18.6 72.8 %collective-permute-start.2 = (bf16[256,1024]{0,1:T(8,128)(2,1)S(1)}, bf16[256,1024]{0,1:T(8,128)(2,1)S(1)}, u32[]{:S(2)}, u32[]{:S(2)}) collective-permute-start(bf16[256,1024]{0,1:T(8,128)(2,1)S(1)} %copy.5), channel_id=1, source_target_pairs={{0,3},{1,2},{2,1},{3,0},{4,7},{5,6},{6,5},{7,4},{8,11},{9,10},{10,... | collective-permute-start | bytes 1572872 | tf_op jit(solution)/shard_map/ppermute | solution.py:178
  133.3 1.6 copy-start.2
  144.6 4.1 %copy-start = (f32[1024,2560]{1,0:T(8,128)}, f32[1024,2560]{1,0:T(8,128)S(1)}, u32[]{:S(2)}) copy-start(f32[1024,2560]{1,0:T(8,128)S(1)} %get-tuple-element.8.old_ref) | copy-start | bytes 31457284
  148.7 14.2 %all-to-all-start.1 = ((f32[32,2,1024]{2,1,0:T(2,128)}), f32[32,2,1024]{2,1,0:T(2,128)S(1)}, u32[]{:S(2)}, u32[]{:S(2)}) async-start(f32[32,2,1024]{2,1,0:T(2,128)} %get-tuple-element.7), calls=%async_computation.1 | async-start | bytes 524288 | tf_op jit(solution)/shard_map/all_to_all | solution.py:184
  162.9 4.0 %copy-start.1 = (f32[1024,2560]{1,0:T(8,128)S(1)}, f32[1024,2560]{1,0:T(8,128)}, u32[]{:S(2)}) copy-start(f32[1024,2560]{1,0:T(8,128)} %copy-done) | copy-start | bytes 31457284
  166.9 1.6 copy-start.3

commit v3 on v2

v3 whole, which is shorter than its diff:
```python
import functools

import jax
import jax.numpy as jnp
from jax import lax
from jax.experimental import pallas as pl
from jax.experimental.pallas import tpu as pltpu
from jax.sharding import PartitionSpec as P

AXES = ("cls", "row")
LANES = 128
LOG2E = 1.4426950408889634
MIB = 1 << 20

learn_rate = 2.0

WHOLE = pl.BlockSpec(memory_space=pltpu.VMEM)
ANYWHERE = pl.BlockSpec(memory_space=pltpu.HBM)


def blocks_of(width):
    step = next(t for t in (512, 256, 128) if width % t == 0)
    widths = [step] * (width // step)
    starts = [sum(widths[:k]) for k in range(len(widths))]
    return [slice(start, start + size) for start, size in zip(starts, widths)]


def diagonal():
    rows = lax.broadcasted_iota(jnp.int32, (LANES, LANES), 0)
    lanes = lax.broadcasted_iota(jnp.int32, (LANES, LANES), 1)
    return rows == lanes


def to_row(column):
    keep = diagonal()
    parts = []
    for start in range(0, column.shape[0], LANES):
        spread = jnp.broadcast_to(column[start : start + LANES], (LANES, LANES))
        parts.append(jnp.sum(jnp.where(keep, spread, 0.0), axis=0, keepdims=True))
    return jnp.concatenate(parts, axis=1)


def to_column(row):
    keep = diagonal()
    parts = []
    for start in range(0, row.shape[1], LANES):
        spread = jnp.broadcast_to(row[:, start : start + LANES], (LANES, LANES))
        parts.append(jnp.sum(jnp.where(keep, spread, 0.0), axis=1, keepdims=True))
    return jnp.concatenate(parts, axis=0)


def combine(masses):
    top = jnp.max(masses, axis=0)
    return top + jnp.log(jnp.sum(jnp.exp2(masses - top[None]), axis=0)) * LOG2E


def tally(logits, hits, first, peak_ref, mass_ref, pick_ref):
    groups = [logits[:, g : g + LANES] for g in range(0, logits.shape[1], LANES)]
    peak = functools.reduce(jnp.maximum, groups)
    if not first:
        peak = jnp.maximum(peak, peak_ref[...])
    mass = functools.reduce(jnp.add, [jnp.exp2(g - peak) for g in groups])
    pick = functools.reduce(jnp.add, [jnp.where(h, g, 0.0) for g, h in zip(groups, hits)])
    if not first:
        mass = mass + mass_ref[...] * jnp.exp2(peak_ref[...] - peak)
        pick = pick + pick_ref[...]
    peak_ref[...] = peak
    mass_ref[...] = mass
    pick_ref[...] = pick


def finish(peak_ref, mass_ref, pick_ref):
    lanes_peak = peak_ref[...]
    peak = jnp.max(lanes_peak, axis=1, keepdims=True)
    mass = jnp.sum(mass_ref[...] * jnp.exp2(lanes_peak - peak), axis=1, keepdims=True)
    pick = jnp.sum(pick_ref[...], axis=1, keepdims=True)
    return to_row(peak + jnp.log(mass) * LOG2E), to_row(pick)


def spread(row, peers):
    return jnp.broadcast_to(row[None], (peers, *row.shape))


def hits_of(places, block):
    lane = lax.broadcasted_iota(jnp.int32, (1, LANES), 1)
    return [places == lane + g for g in range(block.start, block.stop, LANES)]


def onehot(hits):
    return jnp.concatenate([jnp.where(h, 1.0, 0.0) for h in hits], axis=1)


def cast_kernel(in_ref, out_ref):
    width = out_ref.shape[2]
    for k in range(out_ref.shape[0]):
        out_ref[k] = in_ref[:, k * width : (k + 1) * width].astype(out_ref.dtype)


def first_kernel(places_ref, x_ref, w_ref, logits_ref, sent_ref, peak_ref, mass_ref, pick_ref):
    stats = (peak_ref, mass_ref, pick_ref)
    places = places_ref[...]
    depth = x_ref.shape[1]
    for k, block in enumerate(blocks_of(w_ref.shape[2])):
        taken = w_ref[:, :, block].reshape(depth, block.stop - block.start)
        logits = jnp.dot(x_ref[...], taken, preferred_element_type=jnp.float32) * LOG2E
        logits_ref[:, block] = logits
        tally(logits, hits_of(places, block), k == 0, *stats)
    mass, pick = finish(*stats)
    peers, rows = sent_ref.shape[0], x_ref.shape[0]
    share = peers * LANES // rows
    sent_ref[:, :, :rows] = spread(mass, peers)
    for g in range(rows // LANES):
        sent_ref[g * share : (g + 1) * share, :, rows:] = spread(
            pick[:, g * LANES : (g + 1) * LANES], share
        )


def second_kernel(
    got_ref, places_ref, gram_ref, old_ref,
    residual_ref, logits_ref, norm_ref, sent_ref, peak_ref, mass_ref, pick_ref,
):
    rows = old_ref.shape[0]
    stats = (peak_ref, mass_ref, pick_ref)
    log_norm = combine(got_ref[:, :, :rows])
    norm_ref[...] = log_norm
    norm = to_column(log_norm)
    places = places_ref[...]
    blocks = blocks_of(old_ref.shape[1])

    for k, block in enumerate(blocks):
        hits = hits_of(places, block)
        old = old_ref[:, block]
        residual = (jnp.exp2(old - norm) - onehot(hits)).astype(jnp.bfloat16)
        residual_ref[:, block] = residual
        logits = old - jnp.dot(gram_ref[...], residual, preferred_element_type=jnp.float32)
        logits_ref[:, block] = logits
        tally(logits, hits, k == 0, *stats)
    mass, pick = finish(*stats)
    peers = sent_ref.shape[0]
    sent_ref[:, :, :rows] = spread(mass, peers)
    sent_ref[:, :, rows : 2 * rows] = spread(pick, peers)
    sent_ref[:, :, 2 * rows :] = spread(jnp.sum(got_ref[:, :, rows:], axis=0), peers)


def last_kernel(
    norm_ref, got_ref, places_ref, flipped_ref, residual_ref, logits_ref,
    update_hbm, losses_ref, update_ref, sems,
):
    rows = logits_ref.shape[0]
    share = got_ref.shape[0] * LANES // rows
    log_norm = combine(got_ref[:, :, :rows])
    pick = jnp.sum(got_ref[:, :, rows : 2 * rows], axis=0)
    old_pick = jnp.concatenate(
        [got_ref[g * share, :, 2 * rows :] for g in range(rows // LANES)], axis=1
    )
    losses = jnp.concatenate([norm_ref[...] - old_pick, log_norm - pick], axis=0)
    losses_ref[...] = losses * (1.0 / LOG2E)
    norm = to_column(log_norm)
    places = places_ref[...]
    blocks = blocks_of(logits_ref.shape[1])
    slots = update_ref.shape[0]

    def copy(k):
        size = blocks[k].stop - blocks[k].start
        return pltpu.make_async_copy(
            update_ref.at[k % slots, :, pl.ds(0, size)],
            update_hbm.at[:, pl.ds(blocks[k].start, size)],
            sems.at[k % slots],
        )

    for k, block in enumerate(blocks):
        chance = jnp.exp2(logits_ref[:, block] - norm)
        total = residual_ref[:, block].astype(jnp.float32)
        total = total + (chance - onehot(hits_of(places, block)))
        update = jnp.dot(
            flipped_ref[...], total.astype(jnp.bfloat16), preferred_element_type=jnp.float32
        )
        if k >= slots:
            copy(k - slots).wait()
        update_ref[k % slots, :, : block.stop - block.start] = update
        copy(k).start()
    for k in range(max(0, len(blocks) - slots), len(blocks)):
        copy(k).wait()


def grant(mib):
    return pltpu.CompilerParams(vmem_limit_bytes=mib * MIB)


def assemble_kernel(rate, sources_ref, *refs):
    *block_refs, x_ref, gram_ref, flipped_ref = refs
    height = block_refs[0].shape[0]
    for k, block_ref in enumerate(block_refs):
        x_ref[pl.ds(pl.multiple_of(sources_ref[k] * height, height), height), :] = block_ref[...]
    examples = x_ref[...]
    gram = lax.dot_general(
        examples, examples, (((1,), (1,)), ((), ())), preferred_element_type=jnp.float32
    )
    gram_ref[...] = (gram * (rate * LOG2E)).astype(gram_ref.dtype)
    flipped_ref[...] = (examples.T * -rate).astype(flipped_ref.dtype)


def neighbours(block):
    group = lax.axis_size("row")
    mine = lax.axis_index("row")
    paired = group & (group - 1) == 0
    sources, blocks = [mine], [block]
    for k in range(1, group):
        if paired:
            sources.append(mine ^ k)
            hops = [(i, i ^ k) for i in range(group)]
        else:
            sources.append((mine - k) % group)
            hops = [(i, (i + k) % group) for i in range(group)]
        blocks.append(lax.ppermute(block, "row", hops))
    return jnp.stack(sources).astype(jnp.int32), blocks


def near(array):
    return pltpu.with_memory_space_constraint(array, pltpu.VMEM)


def away(array):
    return pltpu.with_memory_space_constraint(array, pltpu.HBM)


def trade(sent):
    return lax.all_to_all(sent, AXES, 0, 0, tiled=True)


def shards(embeddings, weights, labels):
    peers = lax.axis_size(AXES)
    depth = weights.shape[0]
    classes = weights.shape[1] // peers
    f32, bf16 = jnp.float32, jnp.bfloat16
    chunk = 4 if peers % 4 == 0 else 1
    pieces = pl.pallas_call(
        cast_kernel,
        grid=(peers // chunk,),
        in_specs=[pl.BlockSpec((depth, chunk * classes), lambda i: (0, i))],
        out_specs=pl.BlockSpec((chunk, depth, classes), lambda i: (i, 0, 0)),
        out_shape=pltpu.HBM((peers, depth, classes), bf16),
    )(away(weights))
    block = lax.all_to_all(pieces, AXES, 0, 0, tiled=True)

    rows = labels.shape[0]
    rate = learn_rate / rows
    places = labels - lax.axis_index(AXES) * classes
    places = jnp.broadcast_to(places[:, None], (rows, LANES))
    sources, blocks = neighbours(embeddings.astype(bf16))
    examples, gram, flipped = pl.pallas_call(
        functools.partial(assemble_kernel, rate),
        in_specs=[pl.BlockSpec(memory_space=pltpu.SMEM)] + [WHOLE] * len(blocks),
        out_specs=[WHOLE] * 3,
        out_shape=[
            pltpu.VMEM((rows, depth * peers), bf16),
            pltpu.HBM((rows, rows), bf16),
            pltpu.HBM((depth * peers, rows), bf16),
        ],
        compiler_params=grant(16),
    )(sources, *blocks)

    logits_shape = pltpu.VMEM((rows, classes), f32)
    scratch = [pltpu.VMEM((rows, LANES), f32)] * 3
    blocks = blocks_of(classes)
    widest, slots = max(b.stop - b.start for b in blocks), min(3, len(blocks))
    logits, sent = pl.pallas_call(
        first_kernel,
        in_specs=[WHOLE] * 3,
        out_specs=[WHOLE] * 2,
        out_shape=[logits_shape, jax.ShapeDtypeStruct((peers, 1, rows + LANES), f32)],
        scratch_shapes=scratch,
        compiler_params=grant(16),
    )(places, near(examples), near(block))
    residual, logits, norm, sent = pl.pallas_call(
        second_kernel,
        in_specs=[WHOLE] * 4,
        out_specs=[WHOLE] * 4,
        out_shape=[
            pltpu.VMEM((rows, classes), bf16),
            logits_shape,
            jax.ShapeDtypeStruct((1, rows), f32),
            jax.ShapeDtypeStruct((peers, 1, 2 * rows + LANES), f32),
        ],
        scratch_shapes=scratch,
        compiler_params=grant(17),
    )(trade(sent), places, gram, near(logits))
    update, losses = pl.pallas_call(
        last_kernel,
        in_specs=[WHOLE] * 6,
        out_specs=[ANYWHERE, WHOLE],
        out_shape=[
            jax.ShapeDtypeStruct((depth * peers, classes), f32),
            jax.ShapeDtypeStruct((2, rows), f32),
        ],
        scratch_shapes=[
            pltpu.VMEM((slots, depth * peers, widest), f32),
            pltpu.SemaphoreType.DMA((slots,)),
        ],
        compiler_params=grant(16),
    )(norm, trade(sent), places, flipped, near(residual), near(logits))
    return update, losses


def solution(mesh):
    placed = (P("row", None), P(AXES, None), P())
    return jax.shard_map(
        shards,
        mesh=mesh,
        in_specs=placed,
        out_specs=(P(None, AXES), P()),
        check_vma=False,
    )
```

time: 202 us -> 188 us (0.931)
  local copies, waits for them, and re-layouts: 16.8 us -> 3.1 us
  blocking collectives: 12.8 us -> 24.8 us
  waiting for transfers between devices: 116 us -> 108 us
  Pallas kernels: 37.6 us -> 41.5 us
  starting transfers between devices: 13.2 us -> 9.37 us
  matrix products: 3.73 us -> 0 us
    all_to_all x1 -> x2, blocking collectives: 12.8 us -> 24.8 us  [trade(): return lax.all_to_all(sent, AXES, 0, 0, tiled=True)]
    unnamed x13 -> x12, local copies, waits for them, and re-layouts: 11.5 us -> 2.91 us
    all_to_all x1 -> x0, waiting for transfers between devices: 6.67 us -> none  [trade(): return lax.all_to_all(sent, AXES, 0, 0, tiled=True)]
    dynamic_update_slice x5 -> x0, local copies, waits for them, and re-layouts: 4.95 us -> none  [the longest x4 4.88 us: gather_rows(): lax.dynamic_update_slice(whole, lax.ppermute(block, 'row', hops), (source...]
    all_to_all x1, waiting for transfers between devices: 39 us -> 34.8 us  [shards(): block = lax.all_to_all(pieces, AXES, 0, 0, tiled=True)]
    all_to_all x1 -> x0, starting transfers between devices: 3.85 us -> none  [trade(): return lax.all_to_all(sent, AXES, 0, 0, tiled=True)]
    pallas_call x2 -> x3, Pallas kernels: 19.5 us -> 23.2 us  [the longest x1 9.46 us: shards(): pl.pallas_call(second_kernel, in_specs=[WHOLE] * 4, out_specs=[WHOLE] * 4...]
    dot_general x1 -> x0, matrix products: 3.73 us -> none  [shards(): lax.dot_general(examples, examples, (((1,), (1,)), ((), ())), preferred_e...]
  transfers between devices with their start and end apart: 5 -> 4, of which waited for: 4 -> 3; matrix products, arithmetic and copies ran while one was open for 5% -> 0% of each run, Pallas kernels for 0% -> 3%
where the time goes in v3:
time: 188 us
  waiting for transfers between devices  108 us (57%)
  Pallas kernels  41.5 us (22%)
  blocking collectives  24.8 us (13%)
  starting transfers between devices  9.37 us (5%)
  local copies, waits for them, and re-layouts  3.1 us (2%)
    ppermute x3, waiting for transfers between devices, neighbours(): blocks.append(lax.ppermute(block, 'row', hops))  73.4 us
    all_to_all x1, waiting for transfers between devices, shards(): block = lax.all_to_all(pieces, AXES, 0, 0, tiled=True)  34.8 us
    all_to_all x2, blocking collectives, trade(): return lax.all_to_all(sent, AXES, 0, 0, tiled=True)  24.8 us
    pallas_call x1, Pallas kernels, shards(): pl.pallas_call(first_kernel, in_specs=[WHOLE] * 3, out_specs=[WHOLE] * 2,...  9.82 us
    pallas_call x1, Pallas kernels, shards(): pl.pallas_call(second_kernel, in_specs=[WHOLE] * 4, out_specs=[WHOLE] * 4...  9.46 us
    pallas_call x1, Pallas kernels, shards(): pl.pallas_call(last_kernel, in_specs=[WHOLE] * 6, out_specs=[ANYWHERE, WH...  8.77 us
    pallas_call x1, Pallas kernels, shards(): pl.pallas_call(cast_kernel, grid=(peers // chunk,), in_specs=[pl.BlockSpe...  8.43 us
    all_to_all x1, starting transfers between devices, shards(): block = lax.all_to_all(pieces, AXES, 0, 0, tiled=True)  7.44 us
  transfers between devices with their start and end apart: 4, of which 3 were waited for; matrix products, arithmetic and copies ran while one was open for 0% of the time, Pallas kernels for 3%

profile of v3, /device:TPU:0, one launch (start us, length us, event | category | flops | bytes accessed | tf_op | source)
XLA Modules:
  0.0 188.0 jit_solution(13557198982557390800)
XLA Ops:
  0.6 8.4 %shard_map.51 = bf16[32,32,2560]{2,1,0:T(8,128)(2,1)} custom-call(f32[32,81920]{1,0:T(8,128)} %in_ref.1), custom_call_target="tpu_custom_call" | custom-call | tf_op jit(solution)/shard_map/pallas_call | solution.py:237
  9.1 0.0 copy-start.4
  9.1 0.0 copy-start.5
  9.1 7.4 %all-to-all-start = ((bf16[32,32,2560]{2,1,0:T(8,128)(2,1)}), bf16[32,32,2560]{2,1,0:T(8,128)(2,1)}, u32[]{:S(2)}, u32[]{:S(2)}) async-start(bf16[32,32,2560]{2,1,0:T(8,128)(2,1)} %shard_map.51), calls=%async_computation | async-start | bytes 10485760 | tf_op jit(solution)/shard_map/all_to_all | solution.py:244
  16.5 0.0 copy-done.4
  16.5 0.1 convert_element_type.3.refs_0_
  16.6 1.5 collective-permute-start.2
  18.1 0.4 collective-permute-start.1
  18.5 0.0 collective-permute-start
  18.5 0.1 pad_add_fusion.sources_ref
  18.6 0.0 copy-done.5
  18.6 55.1 %collective-permute-done.2.refs_3_ = bf16[256,1024]{1,0:T(8,128)(2,1)S(1)} collective-permute-done((bf16[256,1024]{1,0:T(8,128)(2,1)S(1)}, bf16[256,1024]{1,0:T(8,128)(2,1)S(1)}, u32[]{:S(2)}, u32[]{:S(2)}) %collective-permute-start.2) | collective-permute-done | bytes 524320 | tf_op jit(solution)/shard_map/ppermute | solution.py:215
  73.7 18.3 %collective-permute-done.1.refs_2_ = bf16[256,1024]{1,0:T(8,128)(2,1)S(1)} collective-permute-done((bf16[256,1024]{1,0:T(8,128)(2,1)S(1)}, bf16[256,1024]{1,0:T(8,128)(2,1)S(1)}, u32[]{:S(2)}, u32[]{:S(2)}) %collective-permute-start.1) | collective-permute-done | bytes 524320 | tf_op jit(solution)/shard_map/ppermute | solution.py:215
  92.0 0.0 collective-permute-done.refs_1_
  92.0 5.0 %shard_map.50 = (bf16[1024,1024]{1,0:T(8,128)(2,1)S(1)}, bf16[1024,1024]{1,0:T(8,128)(2,1)}, bf16[1024,1024]{1,0:T(8,128)(2,1)}) custom-call(s32[4]{0:T(128)S(1)} %pad_add_fusion.sources_ref, bf16[256,1024]{1,0:T(8,128)(2,1)S(1)} %convert_element_type.3.refs_0_, bf16[256,1024]{1,0:T(8,128)(2,1)S(1)} %collective-permute-done.refs_1_, ...), custom_call_target="tpu_custom_call" | custom-call | tf_op jit(solution)/shard_map/pallas_call | solution.py:251
  97.0 0.0 copy-start.2
  97.0 1.3 copy-done.2
  98.3 0.0 copy-start.1
  98.3 34.8 %all-to-all-done.w_ref = bf16[32,32,2560]{2,1,0:T(8,128)(2,1)} async-done(((bf16[32,32,2560]{2,1,0:T(8,128)(2,1)}), bf16[32,32,2560]{2,1,0:T(8,128)(2,1)}, u32[]{:S(2)}, u32[]{:S(2)}) %all-to-all-start) | async-done | bytes 5242912 | tf_op jit(solution)/shard_map/all_to_all | solution.py:244
  133.1 0.2 broadcast_in_dim.2.places_ref
  133.3 0.0 copy-start.3
  133.3 1.6 copy-done.3
  134.9 9.8 %shard_map.52 = (f32[1024,2560]{1,0:T(8,128)S(1)}, f32[32,1,1152]{2,1,0:T(1,128)S(1)}) custom-call(s32[1024,128]{1,0:T(8,128)S(1)} %broadcast_in_dim.2.places_ref, bf16[1024,1024]{1,0:T(8,128)(2,1)S(1)} %copy-done.3, bf16[32,32,2560]{2,1,0:T(8,128)(2,1)} %all-to-all-done.w_ref), custom_call_target="tpu_custom_call" | custom-call | tf_op jit(solution)/shard_map/pallas_call | solution.py:267
  144.7 11.9 %all_to_all.15.got_ref = f32[32,1,1152]{2,1,0:T(1,128)S(1)} all-to-all(f32[32,1,1152]{2,1,0:T(1,128)S(1)} %get-tuple-element.12), channel_id=1, replica_groups=mesh['cls'=8,'row'=4] {'cls','row'}, dimensions={0} | all-to-all | bytes 294912 | tf_op jit(solution)/shard_map/all_to_all | solution.py:228
  156.6 0.0 copy-done.1
  156.6 0.0 copy-start
  156.6 9.5 %shard_map.53 = (bf16[1024,2560]{1,0:T(8,128)(2,1)S(1)}, f32[1024,2560]{1,0:T(8,128)S(1)}, f32[1,1024]{1,0:T(1,128)S(1)}, f32[32,1,2176]{2,1,0:T(1,128)S(1)}) custom-call(f32[32,1,1152]{2,1,0:T(1,128)S(1)} %all_to_all.15.got_ref, s32[1024,128]{1,0:T(8,128)S(1)} %broadcast_in_dim.2.places_ref, bf16[1024,1024]{1,0:T(8,128)(2,1)S(1)} %copy-done.1, ...), custom_call_target="tpu_custom_call" | custom-call | tf_op jit(solution)/shard_map/pallas_call | solution.py:275
  166.1 13.0 %all_to_all.16.got_ref = f32[32,1,2176]{2,1,0:T(1,128)S(1)} all-to-all(f32[32,1,2176]{2,1,0:T(1,128)S(1)} %get-tuple-element.16), channel_id=1, replica_groups=mesh['cls'=8,'row'=4] {'cls','row'}, dimensions={0} | all-to-all | bytes 557056 | tf_op jit(solution)/shard_map/all_to_all | solution.py:228
  179.0 0.0 copy-done
  179.0 8.8 %shard_map.54 = (f32[1024,2560]{1,0:T(8,128)}, f32[2,1024]{1,0:T(2,128)}) custom-call(f32[1,1024]{1,0:T(1,128)S(1)} %get-tuple-element.15.norm_ref, f32[32,1,2176]{2,1,0:T(1,128)S(1)} %all_to_all.16.got_ref, s32[1024,128]{1,0:T(8,128)S(1)} %broadcast_in_dim.2.places_ref, bf16[1024,1024]{1,0:T(8,128)(2,1)S(1)} %copy-done, ...), custom_call_target="tpu_custom_call" | custom-call | tf_op jit(solution)/shard_map/pallas_call | solution.py:288
  (1 shorter events, 0.0 us)
Async XLA Ops:
  9.1 7.5 %copy-start.4 = (f32[256,1024]{1,0:T(8,128)S(1)}, f32[256,1024]{1,0:T(8,128)}, u32[]{:S(2)}) copy-start(f32[256,1024]{1,0:T(8,128)} %param.3) | copy-start | bytes 3145732
  9.1 9.5 %copy-start.5 = (s32[1024]{0:T(1024)S(1)}, s32[1024]{0:T(1024)}, u32[]{:S(2)}) copy-start(s32[1024]{0:T(1024)} %param.5) | copy-start | bytes 12292
  9.1 124.0 %all-to-all-start = ((bf16[32,32,2560]{2,1,0:T(8,128)(2,1)}), bf16[32,32,2560]{2,1,0:T(8,128)(2,1)}, u32[]{:S(2)}, u32[]{:S(2)}) async-start(bf16[32,32,2560]{2,1,0:T(8,128)(2,1)} %shard_map.51), calls=%async_computation | async-start | bytes 10485760 | tf_op jit(solution)/shard_map/all_to_all | solution.py:244
  16.6 57.1 %collective-permute-start.2 = (bf16[256,1024]{1,0:T(8,128)(2,1)S(1)}, bf16[256,1024]{1,0:T(8,128)(2,1)S(1)}, u32[]{:S(2)}, u32[]{:S(2)}) collective-permute-start(bf16[256,1024]{1,0:T(8,128)(2,1)S(1)} %convert_element_type.3.refs_0_), channel_id=1, source_target_pairs={{0,3},{1,2},{2,1},{3,0},{4,7},{5,6},{6,5},{7,4},{8,11},{9,10},{10,... | collective-permute-start | bytes 1572872 | tf_op jit(solution)/shard_map/ppermute | solution.py:215
  18.1 73.9 %collective-permute-start.1 = (bf16[256,1024]{1,0:T(8,128)(2,1)S(1)}, bf16[256,1024]{1,0:T(8,128)(2,1)S(1)}, u32[]{:S(2)}, u32[]{:S(2)}) collective-permute-start(bf16[256,1024]{1,0:T(8,128)(2,1)S(1)} %convert_element_type.3.refs_0_), channel_id=1, source_target_pairs={{0,2},{1,3},{2,0},{3,1},{4,6},{5,7},{6,4},{7,5},{8,10},{9,11},{10,... | collective-permute-start | bytes 1572872 | tf_op jit(solution)/shard_map/ppermute | solution.py:215
  18.5 73.5 %collective-permute-start = (bf16[256,1024]{1,0:T(8,128)(2,1)S(1)}, bf16[256,1024]{1,0:T(8,128)(2,1)S(1)}, u32[]{:S(2)}, u32[]{:S(2)}) collective-permute-start(bf16[256,1024]{1,0:T(8,128)(2,1)S(1)} %convert_element_type.3.refs_0_), channel_id=1, source_target_pairs={{0,1},{1,0},{2,3},{3,2},{4,5},{5,4},{6,7},{7,6},{8,9},{9,8},{10,11... | collective-permute-start | bytes 1572872 | tf_op jit(solution)/shard_map/ppermute | solution.py:215
  97.0 1.3 copy-start.2
  98.3 58.3 %copy-start.1 = (bf16[1024,1024]{1,0:T(8,128)(2,1)S(1)}, bf16[1024,1024]{1,0:T(8,128)(2,1)}, u32[]{:S(2)}) copy-start(bf16[1024,1024]{1,0:T(8,128)(2,1)} %get-tuple-element.13.gram_ref) | copy-start | bytes 6291460
  133.3 1.6 copy-start.3
  156.6 22.4 %copy-start = (bf16[1024,1024]{1,0:T(8,128)(2,1)S(1)}, bf16[1024,1024]{1,0:T(8,128)(2,1)}, u32[]{:S(2)}) copy-start(bf16[1024,1024]{1,0:T(8,128)(2,1)} %get-tuple-element.17.flipped_ref) | copy-start | bytes 6291460

commit v4 on v3

--- a/solution.py
+++ b/solution.py
@@ -60,10 +60,11 @@
     if not first:
         peak = jnp.maximum(peak, peak_ref[...])
     mass = functools.reduce(jnp.add, [jnp.exp2(g - peak) for g in groups])
-    pick = functools.reduce(jnp.add, [jnp.where(h, g, 0.0) for g, h in zip(groups, hits)])
+    pick = jnp.zeros_like(peak) if first else pick_ref[...]
+    for g, h in zip(groups, hits):
+        pick = jnp.where(h, g, pick)
     if not first:
         mass = mass + mass_ref[...] * jnp.exp2(peak_ref[...] - peak)
-        pick = pick + pick_ref[...]
     peak_ref[...] = peak
     mass_ref[...] = mass
     pick_ref[...] = pick
@@ -82,7 +83,7 @@
 
 
 def hits_of(places, block):
-    lane = lax.broadcasted_iota(jnp.int32, (1, LANES), 1)
+    lane = lax.broadcasted_iota(jnp.int32, (1, LANES), 1).astype(places.dtype)
     return [places == lane + g for g in range(block.start, block.stop, LANES)]
 
 
@@ -90,17 +91,57 @@
     return jnp.concatenate([jnp.where(h, 1.0, 0.0) for h in hits], axis=1)
 
 
-def cast_kernel(in_ref, out_ref):
-    width = out_ref.shape[2]
-    for k in range(out_ref.shape[0]):
-        out_ref[k] = in_ref[:, k * width : (k + 1) * width].astype(out_ref.dtype)
-
-
-def first_kernel(places_ref, x_ref, w_ref, logits_ref, sent_ref, peak_ref, mass_ref, pick_ref):
+def cast_kernel(in_hbm, out_hbm, wide_ref, slim_ref, in_sems, out_sems):
+    ahead, chunk, _, width = slim_ref.shape
+    steps = out_hbm.shape[0] // chunk
+
+    def load(n):
+        span = pl.ds(n * chunk * width, chunk * width)
+        slot = n % ahead
+        return pltpu.make_async_copy(in_hbm.at[:, span], wide_ref.at[slot], in_sems.at[slot])
+
+    def store(n):
+        slot = n % ahead
+        return pltpu.make_async_copy(
+            slim_ref.at[slot], out_hbm.at[pl.ds(n * chunk, chunk)], out_sems.at[slot]
+        )
+
+    for n in range(min(ahead, steps)):
+        load(n).start()
+    for n in range(steps):
+        load(n).wait()
+        if n >= ahead:
+            store(n - ahead).wait()
+        for k in range(chunk):
+            piece = wide_ref[n % ahead, :, k * width : (k + 1) * width]
+            slim_ref[n % ahead, k] = piece.astype(slim_ref.dtype)
+        store(n).start()
+        if n + ahead < steps:
+            load(n + ahead).start()
+    for n in range(max(0, steps - ahead), steps):
+        store(n).wait()
+
+
+def first_kernel(
+    places_ref, x_hbm, w_hbm, logits_ref, sent_ref, x_ref, w_ref, peak_ref, mass_ref, pick_ref, sems
+):
     stats = (peak_ref, mass_ref, pick_ref)
+    depth = x_ref.shape[1]
+    blocks = blocks_of(w_ref.shape[2])
+    spans = [slice(0, blocks[0].stop), slice(blocks[0].stop, w_ref.shape[2])]
+    copies = [pltpu.make_async_copy(x_hbm, x_ref, sems.at[2])]
+    for n, span in enumerate(spans[: len(blocks)]):
+        part = pl.ds(span.start, span.stop - span.start)
+        copies.append(
+            pltpu.make_async_copy(w_hbm.at[:, :, part], w_ref.at[:, :, part], sems.at[n])
+        )
+    for copy in copies:
+        copy.start()
     places = places_ref[...]
-    depth = x_ref.shape[1]
-    for k, block in enumerate(blocks_of(w_ref.shape[2])):
+    copies[0].wait()
+    for k, block in enumerate(blocks):
+        if k < 2:
+            copies[k + 1].wait()
         taken = w_ref[:, :, block].reshape(depth, block.stop - block.start)
         logits = jnp.dot(x_ref[...], taken, preferred_element_type=jnp.float32) * LOG2E
         logits_ref[:, block] = logits
@@ -132,9 +173,11 @@
         old = old_ref[:, block]
         residual = (jnp.exp2(old - norm) - onehot(hits)).astype(jnp.bfloat16)
         residual_ref[:, block] = residual
-        logits = old - jnp.dot(gram_ref[...], residual, preferred_element_type=jnp.float32)
+        logits = old - jnp.dot(
+            gram_ref[...], residual_ref[:, block], preferred_element_type=jnp.float32
+        )
         logits_ref[:, block] = logits
-        tally(logits, hits, k == 0, *stats)
+        tally(logits, hits_of(places.astype(jnp.float32), block), k == 0, *stats)
     mass, pick = finish(*stats)
     peers = sent_ref.shape[0]
     sent_ref[:, :, :rows] = spread(mass, peers)
@@ -234,12 +277,19 @@
     classes = weights.shape[1] // peers
     f32, bf16 = jnp.float32, jnp.bfloat16
     chunk = 4 if peers % 4 == 0 else 1
+    ahead = min(4, peers // chunk)
     pieces = pl.pallas_call(
         cast_kernel,
-        grid=(peers // chunk,),
-        in_specs=[pl.BlockSpec((depth, chunk * classes), lambda i: (0, i))],
-        out_specs=pl.BlockSpec((chunk, depth, classes), lambda i: (i, 0, 0)),
+        in_specs=[ANYWHERE],
+        out_specs=ANYWHERE,
         out_shape=pltpu.HBM((peers, depth, classes), bf16),
+        scratch_shapes=[
+            pltpu.VMEM((ahead, depth, chunk * classes), f32),
+            pltpu.VMEM((ahead, chunk, depth, classes), bf16),
+            pltpu.SemaphoreType.DMA((ahead,)),
+            pltpu.SemaphoreType.DMA((ahead,)),
+        ],
+        compiler_params=grant(16),
     )(away(weights))
     block = lax.all_to_all(pieces, AXES, 0, 0, tiled=True)
 
@@ -253,7 +303,7 @@
         in_specs=[pl.BlockSpec(memory_space=pltpu.SMEM)] + [WHOLE] * len(blocks),
         out_specs=[WHOLE] * 3,
         out_shape=[
-            pltpu.VMEM((rows, depth * peers), bf16),
+            pltpu.HBM((rows, depth * peers), bf16),
             pltpu.HBM((rows, rows), bf16),
             pltpu.HBM((depth * peers, rows), bf16),
         ],
@@ -266,12 +316,17 @@
     widest, slots = max(b.stop - b.start for b in blocks), min(3, len(blocks))
     logits, sent = pl.pallas_call(
         first_kernel,
-        in_specs=[WHOLE] * 3,
+        in_specs=[WHOLE, ANYWHERE, ANYWHERE],
         out_specs=[WHOLE] * 2,
         out_shape=[logits_shape, jax.ShapeDtypeStruct((peers, 1, rows + LANES), f32)],
-        scratch_shapes=scratch,
+        scratch_shapes=[
+            pltpu.VMEM(examples.shape, bf16),
+            pltpu.VMEM(block.shape, bf16),
+            *scratch,
+            pltpu.SemaphoreType.DMA((3,)),
+        ],
         compiler_params=grant(16),
-    )(places, near(examples), near(block))
+    )(places, away(examples), away(block))
     residual, logits, norm, sent = pl.pallas_call(
         second_kernel,
         in_specs=[WHOLE] * 4,

time: 188 us -> 183 us (0.973)
  Pallas kernels: 41.5 us -> 38.5 us
  local copies, waits for them, and re-layouts: 3.1 us -> 0.21 us
    unnamed x12 -> x8, local copies, waits for them, and re-layouts: 2.91 us -> 0.02 us
    pallas_call x2, Pallas kernels: 18.3 us -> 15.9 us  [the longest x1 9.6 us: shards(): pl.pallas_call(first_kernel, in_specs=[WHOLE, ANYWHERE, ANYWHERE], out_sp...]
where the time goes in v4:
time: 183 us
  waiting for transfers between devices  109 us (60%)
  Pallas kernels  38.5 us (21%)
  blocking collectives  24.8 us (14%)
  starting transfers between devices  9.37 us (5%)
    ppermute x3, waiting for transfers between devices, neighbours(): blocks.append(lax.ppermute(block, 'row', hops))  73.4 us
    all_to_all x1, waiting for transfers between devices, shards(): block = lax.all_to_all(pieces, AXES, 0, 0, tiled=True)  35.9 us
    all_to_all x2, blocking collectives, trade(): return lax.all_to_all(sent, AXES, 0, 0, tiled=True)  24.8 us
    pallas_call x1, Pallas kernels, shards(): pl.pallas_call(first_kernel, in_specs=[WHOLE, ANYWHERE, ANYWHERE], out_sp...  9.6 us
    pallas_call x1, Pallas kernels, shards(): pl.pallas_call(last_kernel, in_specs=[WHOLE] * 6, out_specs=[ANYWHERE, WH...  8.77 us
    pallas_call x1, Pallas kernels, shards(): pl.pallas_call(second_kernel, in_specs=[WHOLE] * 4, out_specs=[WHOLE] * 4...  8.68 us
    all_to_all x1, starting transfers between devices, shards(): block = lax.all_to_all(pieces, AXES, 0, 0, tiled=True)  7.45 us
    pallas_call x1, Pallas kernels, shards(): pl.pallas_call(cast_kernel, in_specs=[ANYWHERE], out_specs=ANYWHERE, out_...  6.29 us
  transfers between devices with their start and end apart: 4, of which 3 were waited for; matrix products, arithmetic and copies ran while one was open for 0% of the time, Pallas kernels for 3%

profile of v4, /device:TPU:0, one launch (start us, length us, event | category | flops | bytes accessed | tf_op | source)
XLA Modules:
  0.0 183.3 jit_solution(11191930687607104163)
XLA Ops:
  0.6 6.3 %shard_map.51 = bf16[32,32,2560]{2,1,0:T(8,128)(2,1)} custom-call(f32[32,81920]{1,0:T(8,128)} %in_hbm.1), custom_call_target="tpu_custom_call" | custom-call | tf_op jit(solution)/shard_map/pallas_call | solution.py:281
  6.9 0.0 copy-start.2
  6.9 0.0 copy-start.3
  7.0 7.4 %all-to-all-start = ((bf16[32,32,2560]{2,1,0:T(8,128)(2,1)}), bf16[32,32,2560]{2,1,0:T(8,128)(2,1)}, u32[]{:S(2)}, u32[]{:S(2)}) async-start(bf16[32,32,2560]{2,1,0:T(8,128)(2,1)} %shard_map.51), calls=%async_computation | async-start | bytes 10485760 | tf_op jit(solution)/shard_map/all_to_all | solution.py:294
  14.4 0.0 copy-done.2
  14.4 0.1 convert_element_type.3.refs_0_
  14.5 1.5 collective-permute-start.2
  16.0 0.4 collective-permute-start.1
  16.4 0.0 collective-permute-start
  16.4 0.1 pad_add_fusion.sources_ref
  16.5 0.0 copy-done.3
  16.5 55.1 %collective-permute-done.2.refs_3_ = bf16[256,1024]{1,0:T(8,128)(2,1)S(1)} collective-permute-done((bf16[256,1024]{1,0:T(8,128)(2,1)S(1)}, bf16[256,1024]{1,0:T(8,128)(2,1)S(1)}, u32[]{:S(2)}, u32[]{:S(2)}) %collective-permute-start.2) | collective-permute-done | bytes 524320 | tf_op jit(solution)/shard_map/ppermute | solution.py:258
  71.6 18.3 %collective-permute-done.1.refs_2_ = bf16[256,1024]{1,0:T(8,128)(2,1)S(1)} collective-permute-done((bf16[256,1024]{1,0:T(8,128)(2,1)S(1)}, bf16[256,1024]{1,0:T(8,128)(2,1)S(1)}, u32[]{:S(2)}, u32[]{:S(2)}) %collective-permute-start.1) | collective-permute-done | bytes 524320 | tf_op jit(solution)/shard_map/ppermute | solution.py:258
  89.9 0.0 collective-permute-done.refs_1_
  89.9 5.2 %shard_map.50 = (bf16[1024,1024]{1,0:T(8,128)(2,1)}, bf16[1024,1024]{1,0:T(8,128)(2,1)}, bf16[1024,1024]{1,0:T(8,128)(2,1)}) custom-call(s32[4]{0:T(128)S(1)} %pad_add_fusion.sources_ref, bf16[256,1024]{1,0:T(8,128)(2,1)S(1)} %convert_element_type.3.refs_0_, bf16[256,1024]{1,0:T(8,128)(2,1)S(1)} %collective-permute-done.refs_1_, ...), custom_call_target="tpu_custom_call" | custom-call | tf_op jit(solution)/shard_map/pallas_call | solution.py:301
  95.0 0.0 copy-start.1
  95.0 35.9 %all-to-all-done.w_hbm = bf16[32,32,2560]{2,1,0:T(8,128)(2,1)} async-done(((bf16[32,32,2560]{2,1,0:T(8,128)(2,1)}), bf16[32,32,2560]{2,1,0:T(8,128)(2,1)}, u32[]{:S(2)}, u32[]{:S(2)}) %all-to-all-start) | async-done | bytes 5242912 | tf_op jit(solution)/shard_map/all_to_all | solution.py:294
  131.0 0.2 broadcast_in_dim.2.places_ref
  131.2 9.6 %shard_map.52 = (f32[1024,2560]{1,0:T(8,128)S(1)}, f32[32,1,1152]{2,1,0:T(1,128)S(1)}) custom-call(s32[1024,128]{1,0:T(8,128)S(1)} %broadcast_in_dim.2.places_ref, bf16[1024,1024]{1,0:T(8,128)(2,1)} %get-tuple-element.11.x_hbm, bf16[32,32,2560]{2,1,0:T(8,128)(2,1)} %all-to-all-done.w_hbm), custom_call_target="tpu_custom_call" | custom-call | tf_op jit(solution)/shard_map/pallas_call | solution.py:317
  140.8 11.9 %all_to_all.15.got_ref = f32[32,1,1152]{2,1,0:T(1,128)S(1)} all-to-all(f32[32,1,1152]{2,1,0:T(1,128)S(1)} %get-tuple-element.12), channel_id=1, replica_groups=mesh['cls'=8,'row'=4] {'cls','row'}, dimensions={0} | all-to-all | bytes 294912 | tf_op jit(solution)/shard_map/all_to_all | solution.py:271
  152.7 0.0 copy-done.1
  152.7 0.0 copy-start
  152.7 8.7 %shard_map.53 = (bf16[1024,2560]{1,0:T(8,128)(2,1)S(1)}, f32[1024,2560]{1,0:T(8,128)S(1)}, f32[1,1024]{1,0:T(1,128)S(1)}, f32[32,1,2176]{2,1,0:T(1,128)S(1)}) custom-call(f32[32,1,1152]{2,1,0:T(1,128)S(1)} %all_to_all.15.got_ref, s32[1024,128]{1,0:T(8,128)S(1)} %broadcast_in_dim.2.places_ref, bf16[1024,1024]{1,0:T(8,128)(2,1)S(1)} %copy-done.1, ...), custom_call_target="tpu_custom_call" | custom-call | tf_op jit(solution)/shard_map/pallas_call | solution.py:330
  161.4 13.0 %all_to_all.16.got_ref = f32[32,1,2176]{2,1,0:T(1,128)S(1)} all-to-all(f32[32,1,2176]{2,1,0:T(1,128)S(1)} %get-tuple-element.16), channel_id=1, replica_groups=mesh['cls'=8,'row'=4] {'cls','row'}, dimensions={0} | all-to-all | bytes 557056 | tf_op jit(solution)/shard_map/all_to_all | solution.py:271
  174.3 0.0 copy-done
  174.3 8.8 %shard_map.54 = (f32[1024,2560]{1,0:T(8,128)}, f32[2,1024]{1,0:T(2,128)}) custom-call(f32[1,1024]{1,0:T(1,128)S(1)} %get-tuple-element.15.norm_ref, f32[32,1,2176]{2,1,0:T(1,128)S(1)} %all_to_all.16.got_ref, s32[1024,128]{1,0:T(8,128)S(1)} %broadcast_in_dim.2.places_ref, bf16[1024,1024]{1,0:T(8,128)(2,1)S(1)} %copy-done, ...), custom_call_target="tpu_custom_call" | custom-call | tf_op jit(solution)/shard_map/pallas_call | solution.py:343
  (1 shorter events, 0.0 us)
Async XLA Ops:
  6.9 7.5 %copy-start.2 = (f32[256,1024]{1,0:T(8,128)S(1)}, f32[256,1024]{1,0:T(8,128)}, u32[]{:S(2)}) copy-start(f32[256,1024]{1,0:T(8,128)} %param.3) | copy-start | bytes 3145732
  6.9 9.6 %copy-start.3 = (s32[1024]{0:T(1024)S(1)}, s32[1024]{0:T(1024)}, u32[]{:S(2)}) copy-start(s32[1024]{0:T(1024)} %param.5) | copy-start | bytes 12292
  7.0 124.0 %all-to-all-start = ((bf16[32,32,2560]{2,1,0:T(8,128)(2,1)}), bf16[32,32,2560]{2,1,0:T(8,128)(2,1)}, u32[]{:S(2)}, u32[]{:S(2)}) async-start(bf16[32,32,2560]{2,1,0:T(8,128)(2,1)} %shard_map.51), calls=%async_computation | async-start | bytes 10485760 | tf_op jit(solution)/shard_map/all_to_all | solution.py:294
  14.5 57.1 %collective-permute-start.2 = (bf16[256,1024]{1,0:T(8,128)(2,1)S(1)}, bf16[256,1024]{1,0:T(8,128)(2,1)S(1)}, u32[]{:S(2)}, u32[]{:S(2)}) collective-permute-start(bf16[256,1024]{1,0:T(8,128)(2,1)S(1)} %convert_element_type.3.refs_0_), channel_id=1, source_target_pairs={{0,3},{1,2},{2,1},{3,0},{4,7},{5,6},{6,5},{7,4},{8,11},{9,10},{10,... | collective-permute-start | bytes 1572872 | tf_op jit(solution)/shard_map/ppermute | solution.py:258
  16.0 73.9 %collective-permute-start.1 = (bf16[256,1024]{1,0:T(8,128)(2,1)S(1)}, bf16[256,1024]{1,0:T(8,128)(2,1)S(1)}, u32[]{:S(2)}, u32[]{:S(2)}) collective-permute-start(bf16[256,1024]{1,0:T(8,128)(2,1)S(1)} %convert_element_type.3.refs_0_), channel_id=1, source_target_pairs={{0,2},{1,3},{2,0},{3,1},{4,6},{5,7},{6,4},{7,5},{8,10},{9,11},{10,... | collective-permute-start | bytes 1572872 | tf_op jit(solution)/shard_map/ppermute | solution.py:258
  16.4 73.5 %collective-permute-start = (bf16[256,1024]{1,0:T(8,128)(2,1)S(1)}, bf16[256,1024]{1,0:T(8,128)(2,1)S(1)}, u32[]{:S(2)}, u32[]{:S(2)}) collective-permute-start(bf16[256,1024]{1,0:T(8,128)(2,1)S(1)} %convert_element_type.3.refs_0_), channel_id=1, source_target_pairs={{0,1},{1,0},{2,3},{3,2},{4,5},{5,4},{6,7},{7,6},{8,9},{9,8},{10,11... | collective-permute-start | bytes 1572872 | tf_op jit(solution)/shard_map/ppermute | solution.py:258
  95.0 57.6 %copy-start.1 = (bf16[1024,1024]{1,0:T(8,128)(2,1)S(1)}, bf16[1024,1024]{1,0:T(8,128)(2,1)}, u32[]{:S(2)}) copy-start(bf16[1024,1024]{1,0:T(8,128)(2,1)} %get-tuple-element.13.gram_ref) | copy-start | bytes 6291460
  152.7 21.7 %copy-start = (bf16[1024,1024]{1,0:T(8,128)(2,1)S(1)}, bf16[1024,1024]{1,0:T(8,128)(2,1)}, u32[]{:S(2)}) copy-start(bf16[1024,1024]{1,0:T(8,128)(2,1)} %get-tuple-element.17.flipped_ref) | copy-start | bytes 6291460

commit v5 on v4

--- a/solution.py
+++ b/solution.py
@@ -82,9 +82,14 @@
     return jnp.broadcast_to(row[None], (peers, *row.shape))
 
 
-def hits_of(places, block):
-    lane = lax.broadcasted_iota(jnp.int32, (1, LANES), 1).astype(places.dtype)
-    return [places == lane + g for g in range(block.start, block.stop, LANES)]
+def hits_of(places, columns_ref, block):
+    rows = places.shape[0]
+    places = places.reshape(rows // 8, 8, LANES)
+    starts = range(block.start, block.stop, LANES)
+    return [
+        (places == columns_ref[:, g : g + LANES][None]).reshape(rows, LANES)
+        for g in starts
+    ]
 
 
 def onehot(hits):
@@ -123,7 +128,7 @@
 
 
 def first_kernel(
-    places_ref, x_hbm, w_hbm, logits_ref, sent_ref, x_ref, w_ref, peak_ref, mass_ref, pick_ref, sems
+    places_ref, columns_ref, x_hbm, w_hbm, logits_ref, sent_ref, x_ref, w_ref, peak_ref, mass_ref, pick_ref, sems
 ):
     stats = (peak_ref, mass_ref, pick_ref)
     depth = x_ref.shape[1]
@@ -145,7 +150,9 @@
         taken = w_ref[:, :, block].reshape(depth, block.stop - block.start)
         logits = jnp.dot(x_ref[...], taken, preferred_element_type=jnp.float32) * LOG2E
         logits_ref[:, block] = logits
-        tally(logits, hits_of(places, block), k == 0, *stats)
+        if k % 2 or k == len(blocks) - 1:
+            both = slice(blocks[k - k % 2].start, block.stop)
+            tally(logits_ref[:, both], hits_of(places, columns_ref, both), k < 2, *stats)
     mass, pick = finish(*stats)
     peers, rows = sent_ref.shape[0], x_ref.shape[0]
     share = peers * LANES // rows
@@ -157,7 +164,7 @@
 
 
 def second_kernel(
-    got_ref, places_ref, gram_ref, old_ref,
+    got_ref, places_ref, columns_ref, floats_ref, gram_ref, old_ref,
     residual_ref, logits_ref, norm_ref, sent_ref, peak_ref, mass_ref, pick_ref,
 ):
     rows = old_ref.shape[0]
@@ -166,10 +173,11 @@
     norm_ref[...] = log_norm
     norm = to_column(log_norm)
     places = places_ref[...]
+    labels = places.astype(jnp.float32)
     blocks = blocks_of(old_ref.shape[1])
 
     for k, block in enumerate(blocks):
-        hits = hits_of(places, block)
+        hits = hits_of(places, columns_ref, block)
         old = old_ref[:, block]
         residual = (jnp.exp2(old - norm) - onehot(hits)).astype(jnp.bfloat16)
         residual_ref[:, block] = residual
@@ -177,7 +185,9 @@
             gram_ref[...], residual_ref[:, block], preferred_element_type=jnp.float32
         )
         logits_ref[:, block] = logits
-        tally(logits, hits_of(places.astype(jnp.float32), block), k == 0, *stats)
+        if k % 2 or k == len(blocks) - 1:
+            both = slice(blocks[k - k % 2].start, block.stop)
+            tally(logits_ref[:, both], hits_of(labels, floats_ref, both), k < 2, *stats)
     mass, pick = finish(*stats)
     peers = sent_ref.shape[0]
     sent_ref[:, :, :rows] = spread(mass, peers)
@@ -186,7 +196,7 @@
 
 
 def last_kernel(
-    norm_ref, got_ref, places_ref, flipped_ref, residual_ref, logits_ref,
+    norm_ref, got_ref, places_ref, columns_ref, flipped_ref, residual_ref, logits_ref,
     update_hbm, losses_ref, update_ref, sems,
 ):
     rows = logits_ref.shape[0]
@@ -214,7 +224,7 @@
     for k, block in enumerate(blocks):
         chance = jnp.exp2(logits_ref[:, block] - norm)
         total = residual_ref[:, block].astype(jnp.float32)
-        total = total + (chance - onehot(hits_of(places, block)))
+        total = total + (chance - onehot(hits_of(places, columns_ref, block)))
         update = jnp.dot(
             flipped_ref[...], total.astype(jnp.bfloat16), preferred_element_type=jnp.float32
         )
@@ -310,13 +320,15 @@
         compiler_params=grant(16),
     )(sources, *blocks)
 
+    columns = lax.broadcasted_iota(jnp.int32, (8, classes), 1)
+    places, columns, floats = lax.optimization_barrier((places, columns, columns.astype(f32)))
     logits_shape = pltpu.VMEM((rows, classes), f32)
     scratch = [pltpu.VMEM((rows, LANES), f32)] * 3
     blocks = blocks_of(classes)
     widest, slots = max(b.stop - b.start for b in blocks), min(3, len(blocks))
     logits, sent = pl.pallas_call(
         first_kernel,
-        in_specs=[WHOLE, ANYWHERE, ANYWHERE],
+        in_specs=[WHOLE, WHOLE, ANYWHERE, ANYWHERE],
         out_specs=[WHOLE] * 2,
         out_shape=[logits_shape, jax.ShapeDtypeStruct((peers, 1, rows + LANES), f32)],
         scratch_shapes=[
@@ -326,10 +338,10 @@
             pltpu.SemaphoreType.DMA((3,)),
         ],
         compiler_params=grant(16),
-    )(places, away(examples), away(block))
+    )(places, columns, away(examples), away(block))
     residual, logits, norm, sent = pl.pallas_call(
         second_kernel,
-        in_specs=[WHOLE] * 4,
+        in_specs=[WHOLE] * 6,
         out_specs=[WHOLE] * 4,
         out_shape=[
             pltpu.VMEM((rows, classes), bf16),
@@ -339,10 +351,10 @@
         ],
         scratch_shapes=scratch,
         compiler_params=grant(17),
-    )(trade(sent), places, gram, near(logits))
+    )(trade(sent), places, columns, floats, gram, near(logits))
     update, losses = pl.pallas_call(
         last_kernel,
-        in_specs=[WHOLE] * 6,
+        in_specs=[WHOLE] * 7,
         out_specs=[ANYWHERE, WHOLE],
         out_shape=[
             jax.ShapeDtypeStruct((depth * peers, classes), f32),
@@ -353,7 +365,7 @@
             pltpu.SemaphoreType.DMA((slots,)),
         ],
         compiler_params=grant(16),
-    )(norm, trade(sent), places, flipped, near(residual), near(logits))
+    )(norm, trade(sent), places, columns, flipped, near(residual), near(logits))
     return update, losses
 
 

time: 183 us -> 182 us (level)
  no operation moved by 1% of the time
where the time goes in v5:
time: 182 us
  waiting for transfers between devices  109 us (60%)
  Pallas kernels  37.6 us (21%)
  blocking collectives  24.9 us (14%)
  starting transfers between devices  9.37 us (5%)
    ppermute x3, waiting for transfers between devices, neighbours(): blocks.append(lax.ppermute(block, 'row', hops))  73.1 us
    all_to_all x1, waiting for transfers between devices, shards(): block = lax.all_to_all(pieces, AXES, 0, 0, tiled=True)  35.9 us
    all_to_all x2, blocking collectives, trade(): return lax.all_to_all(sent, AXES, 0, 0, tiled=True)  24.9 us
    pallas_call x1, Pallas kernels, shards(): pl.pallas_call(first_kernel, in_specs=[WHOLE, WHOLE, ANYWHERE, ANYWHERE],...  9.32 us
    pallas_call x1, Pallas kernels, shards(): pl.pallas_call(last_kernel, in_specs=[WHOLE] * 7, out_specs=[ANYWHERE, WH...  8.64 us
    pallas_call x1, Pallas kernels, shards(): pl.pallas_call(second_kernel, in_specs=[WHOLE] * 6, out_specs=[WHOLE] * 4...  8.15 us
    all_to_all x1, starting transfers between devices, shards(): block = lax.all_to_all(pieces, AXES, 0, 0, tiled=True)  7.45 us
    pallas_call x1, Pallas kernels, shards(): pl.pallas_call(cast_kernel, in_specs=[ANYWHERE], out_specs=ANYWHERE, out_...  6.29 us
  transfers between devices with their start and end apart: 4, of which 3 were waited for; matrix products, arithmetic and copies ran while one was open for 0% of the time, Pallas kernels for 3%

profile of v5, /device:TPU:0, one launch (start us, length us, event | category | flops | bytes accessed | tf_op | source)
XLA Modules:
  0.0 182.2 jit_solution(616136939515761375)
XLA Ops:
  0.6 6.3 %shard_map.51 = bf16[32,32,2560]{2,1,0:T(8,128)(2,1)} custom-call(f32[32,81920]{1,0:T(8,128)} %in_hbm.1), custom_call_target="tpu_custom_call" | custom-call | tf_op jit(solution)/shard_map/pallas_call | solution.py:291
  6.9 0.0 copy-start.2
  6.9 0.0 copy-start.3
  7.0 7.4 %all-to-all-start = ((bf16[32,32,2560]{2,1,0:T(8,128)(2,1)}), bf16[32,32,2560]{2,1,0:T(8,128)(2,1)}, u32[]{:S(2)}, u32[]{:S(2)}) async-start(bf16[32,32,2560]{2,1,0:T(8,128)(2,1)} %shard_map.51), calls=%async_computation | async-start | bytes 10485760 | tf_op jit(solution)/shard_map/all_to_all | solution.py:304
  14.4 0.0 copy-done.2
  14.4 0.1 convert_element_type.8.refs_0_
  14.5 1.5 collective-permute-start.2
  16.0 0.4 collective-permute-start.1
  16.4 0.0 collective-permute-start
  16.4 0.0 copy-done.3
  16.5 0.2 broadcast_in_dim.2.places_ref
  16.7 0.1 pad_add_fusion.sources_ref
  16.7 54.8 %collective-permute-done.2.refs_3_ = bf16[256,1024]{1,0:T(8,128)(2,1)S(1)} collective-permute-done((bf16[256,1024]{1,0:T(8,128)(2,1)S(1)}, bf16[256,1024]{1,0:T(8,128)(2,1)S(1)}, u32[]{:S(2)}, u32[]{:S(2)}) %collective-permute-start.2) | collective-permute-done | bytes 524320 | tf_op jit(solution)/shard_map/ppermute | solution.py:268
  71.6 18.3 %collective-permute-done.1.refs_2_ = bf16[256,1024]{1,0:T(8,128)(2,1)S(1)} collective-permute-done((bf16[256,1024]{1,0:T(8,128)(2,1)S(1)}, bf16[256,1024]{1,0:T(8,128)(2,1)S(1)}, u32[]{:S(2)}, u32[]{:S(2)}) %collective-permute-start.1) | collective-permute-done | bytes 524320 | tf_op jit(solution)/shard_map/ppermute | solution.py:268
  89.9 0.0 collective-permute-done.refs_1_
  89.9 5.2 %shard_map.50 = (bf16[1024,1024]{1,0:T(8,128)(2,1)}, bf16[1024,1024]{1,0:T(8,128)(2,1)}, bf16[1024,1024]{1,0:T(8,128)(2,1)}) custom-call(s32[4]{0:T(128)S(1)} %pad_add_fusion.sources_ref, bf16[256,1024]{1,0:T(8,128)(2,1)S(1)} %convert_element_type.8.refs_0_, bf16[256,1024]{1,0:T(8,128)(2,1)S(1)} %collective-permute-done.refs_1_, ...), custom_call_target="tpu_custom_call" | custom-call | tf_op jit(solution)/shard_map/pallas_call | solution.py:311
  95.0 0.0 copy-start.1
  95.0 35.9 %all-to-all-done.w_hbm = bf16[32,32,2560]{2,1,0:T(8,128)(2,1)} async-done(((bf16[32,32,2560]{2,1,0:T(8,128)(2,1)}), bf16[32,32,2560]{2,1,0:T(8,128)(2,1)}, u32[]{:S(2)}, u32[]{:S(2)}) %all-to-all-start) | async-done | bytes 5242912 | tf_op jit(solution)/shard_map/all_to_all | solution.py:304
  131.0 9.3 %shard_map.52 = (f32[1024,2560]{1,0:T(8,128)S(1)}, f32[32,1,1152]{2,1,0:T(1,128)S(1)}) custom-call(s32[1024,128]{1,0:T(8,128)S(1)} %broadcast_in_dim.2.places_ref, s32[8,2560]{1,0:T(8,128)S(1)} %iota.9.columns_ref, bf16[1024,1024]{1,0:T(8,128)(2,1)} %get-tuple-element.16.x_hbm, bf16[32,32,2560]{2,1,0:T(8,128)(2,1)} %all-to-all-done.w_hbm), custom_call_target="tpu_custom_call" | custom-call | tf_op jit(solution)/shard_map/pallas_call | solution.py:329
  140.3 11.9 %all_to_all.15.got_ref = f32[32,1,1152]{2,1,0:T(1,128)S(1)} all-to-all(f32[32,1,1152]{2,1,0:T(1,128)S(1)} %get-tuple-element.17), channel_id=1, replica_groups=mesh['cls'=8,'row'=4] {'cls','row'}, dimensions={0} | all-to-all | bytes 294912 | tf_op jit(solution)/shard_map/all_to_all | solution.py:281
  152.2 0.0 copy-done.1
  152.2 0.0 copy-start
  152.2 8.2 %shard_map.53 = (bf16[1024,2560]{1,0:T(8,128)(2,1)S(1)}, f32[1024,2560]{1,0:T(8,128)S(1)}, f32[1,1024]{1,0:T(1,128)S(1)}, f32[32,1,2176]{2,1,0:T(1,128)S(1)}) custom-call(f32[32,1,1152]{2,1,0:T(1,128)S(1)} %all_to_all.15.got_ref, s32[1024,128]{1,0:T(8,128)S(1)} %broadcast_in_dim.2.places_ref, s32[8,2560]{1,0:T(8,128)S(1)} %iota.9.columns_ref, ...), custom_call_target="tpu_custom_call" | custom-call | tf_op jit(solution)/shard_map/pallas_call | solution.py:342
  160.4 13.0 %all_to_all.16.got_ref = f32[32,1,2176]{2,1,0:T(1,128)S(1)} all-to-all(f32[32,1,2176]{2,1,0:T(1,128)S(1)} %get-tuple-element.22), channel_id=1, replica_groups=mesh['cls'=8,'row'=4] {'cls','row'}, dimensions={0} | all-to-all | bytes 557056 | tf_op jit(solution)/shard_map/all_to_all | solution.py:281
  173.3 0.0 copy-done
  173.3 8.6 %shard_map.54 = (f32[1024,2560]{1,0:T(8,128)}, f32[2,1024]{1,0:T(2,128)}) custom-call(f32[1,1024]{1,0:T(1,128)S(1)} %get-tuple-element.21.norm_ref, f32[32,1,2176]{2,1,0:T(1,128)S(1)} %all_to_all.16.got_ref, s32[1024,128]{1,0:T(8,128)S(1)} %broadcast_in_dim.2.places_ref, s32[8,2560]{1,0:T(8,128)S(1)} %iota.9.columns_ref, bf16[1024,1024]{1,0:T(8,128)(2,1)S(1)} %copy-done, ...), custom_call_target="tpu_custom_call" | custom-call | tf_op jit(solution)/shard_map/pallas_call | solution.py:355
  (4 shorter events, 0.0 us)
Async XLA Ops:
  6.9 7.5 %copy-start.2 = (f32[256,1024]{1,0:T(8,128)S(1)}, f32[256,1024]{1,0:T(8,128)}, u32[]{:S(2)}) copy-start(f32[256,1024]{1,0:T(8,128)} %param.3) | copy-start | bytes 3145732
  6.9 9.5 %copy-start.3 = (s32[1024]{0:T(1024)S(1)}, s32[1024]{0:T(1024)}, u32[]{:S(2)}) copy-start(s32[1024]{0:T(1024)} %param.5) | copy-start | bytes 12292
  7.0 124.0 %all-to-all-start = ((bf16[32,32,2560]{2,1,0:T(8,128)(2,1)}), bf16[32,32,2560]{2,1,0:T(8,128)(2,1)}, u32[]{:S(2)}, u32[]{:S(2)}) async-start(bf16[32,32,2560]{2,1,0:T(8,128)(2,1)} %shard_map.51), calls=%async_computation | async-start | bytes 10485760 | tf_op jit(solution)/shard_map/all_to_all | solution.py:304
  14.5 57.1 %collective-permute-start.2 = (bf16[256,1024]{1,0:T(8,128)(2,1)S(1)}, bf16[256,1024]{1,0:T(8,128)(2,1)S(1)}, u32[]{:S(2)}, u32[]{:S(2)}) collective-permute-start(bf16[256,1024]{1,0:T(8,128)(2,1)S(1)} %convert_element_type.8.refs_0_), channel_id=1, source_target_pairs={{0,3},{1,2},{2,1},{3,0},{4,7},{5,6},{6,5},{7,4},{8,11},{9,10},{10,... | collective-permute-start | bytes 1572872 | tf_op jit(solution)/shard_map/ppermute | solution.py:268
  16.0 73.9 %collective-permute-start.1 = (bf16[256,1024]{1,0:T(8,128)(2,1)S(1)}, bf16[256,1024]{1,0:T(8,128)(2,1)S(1)}, u32[]{:S(2)}, u32[]{:S(2)}) collective-permute-start(bf16[256,1024]{1,0:T(8,128)(2,1)S(1)} %convert_element_type.8.refs_0_), channel_id=1, source_target_pairs={{0,2},{1,3},{2,0},{3,1},{4,6},{5,7},{6,4},{7,5},{8,10},{9,11},{10,... | collective-permute-start | bytes 1572872 | tf_op jit(solution)/shard_map/ppermute | solution.py:268
  16.4 73.5 %collective-permute-start = (bf16[256,1024]{1,0:T(8,128)(2,1)S(1)}, bf16[256,1024]{1,0:T(8,128)(2,1)S(1)}, u32[]{:S(2)}, u32[]{:S(2)}) collective-permute-start(bf16[256,1024]{1,0:T(8,128)(2,1)S(1)} %convert_element_type.8.refs_0_), channel_id=1, source_target_pairs={{0,1},{1,0},{2,3},{3,2},{4,5},{5,4},{6,7},{7,6},{8,9},{9,8},{10,11... | collective-permute-start | bytes 1572872 | tf_op jit(solution)/shard_map/ppermute | solution.py:268
  95.0 57.2 %copy-start.1 = (bf16[1024,1024]{1,0:T(8,128)(2,1)S(1)}, bf16[1024,1024]{1,0:T(8,128)(2,1)}, u32[]{:S(2)}) copy-start(bf16[1024,1024]{1,0:T(8,128)(2,1)} %get-tuple-element.19.gram_ref) | copy-start | bytes 6291460
  152.2 21.1 %copy-start = (bf16[1024,1024]{1,0:T(8,128)(2,1)S(1)}, bf16[1024,1024]{1,0:T(8,128)(2,1)}, u32[]{:S(2)}) copy-start(bf16[1024,1024]{1,0:T(8,128)(2,1)} %get-tuple-element.23.flipped_ref) | copy-start | bytes 6291460

commit v6 on v5

--- a/solution.py
+++ b/solution.py
@@ -23,6 +23,12 @@
     widths = [step] * (width // step)
     starts = [sum(widths[:k]) for k in range(len(widths))]
     return [slice(start, start + size) for start, size in zip(starts, widths)]
+
+
+def wide_blocks(width):
+    blocks = blocks_of(width)
+    pairs = [blocks[k : k + 2] for k in range(0, len(blocks), 2)]
+    return [slice(pair[0].start, pair[-1].stop) for pair in pairs]
 
 
 def diagonal():
@@ -210,7 +216,7 @@
     losses_ref[...] = losses * (1.0 / LOG2E)
     norm = to_column(log_norm)
     places = places_ref[...]
-    blocks = blocks_of(logits_ref.shape[1])
+    blocks = wide_blocks(logits_ref.shape[1])
     slots = update_ref.shape[0]
 
     def copy(k):
@@ -325,7 +331,8 @@
     logits_shape = pltpu.VMEM((rows, classes), f32)
     scratch = [pltpu.VMEM((rows, LANES), f32)] * 3
     blocks = blocks_of(classes)
-    widest, slots = max(b.stop - b.start for b in blocks), min(3, len(blocks))
+    wide = wide_blocks(classes)
+    widest, slots = max(b.stop - b.start for b in wide), min(2, len(wide))
     logits, sent = pl.pallas_call(
         first_kernel,
         in_specs=[WHOLE, WHOLE, ANYWHERE, ANYWHERE],
@@ -364,7 +371,7 @@
             pltpu.VMEM((slots, depth * peers, widest), f32),
             pltpu.SemaphoreType.DMA((slots,)),
         ],
-        compiler_params=grant(16),
+        compiler_params=grant(18),
     )(norm, trade(sent), places, columns, flipped, near(residual), near(logits))
     return update, losses
 

time: 182 us -> 182 us (level)
  no operation moved by 1% of the time
where the time goes in v6:
time: 182 us
  waiting for transfers between devices  109 us (60%)
  Pallas kernels  37.4 us (21%)
  blocking collectives  24.9 us (14%)
  starting transfers between devices  9.37 us (5%)
    ppermute x3, waiting for transfers between devices, neighbours(): blocks.append(lax.ppermute(block, 'row', hops))  73.1 us
    all_to_all x1, waiting for transfers between devices, shards(): block = lax.all_to_all(pieces, AXES, 0, 0, tiled=True)  35.9 us
    all_to_all x2, blocking collectives, trade(): return lax.all_to_all(sent, AXES, 0, 0, tiled=True)  24.9 us
    pallas_call x1, Pallas kernels, shards(): pl.pallas_call(first_kernel, in_specs=[WHOLE, WHOLE, ANYWHERE, ANYWHERE],...  9.32 us
    pallas_call x1, Pallas kernels, shards(): pl.pallas_call(last_kernel, in_specs=[WHOLE] * 7, out_specs=[ANYWHERE, WH...  8.43 us
    pallas_call x1, Pallas kernels, shards(): pl.pallas_call(second_kernel, in_specs=[WHOLE] * 6, out_specs=[WHOLE] * 4...  8.15 us
    all_to_all x1, starting transfers between devices, shards(): block = lax.all_to_all(pieces, AXES, 0, 0, tiled=True)  7.45 us
    pallas_call x1, Pallas kernels, shards(): pl.pallas_call(cast_kernel, in_specs=[ANYWHERE], out_specs=ANYWHERE, out_...  6.29 us
  transfers between devices with their start and end apart: 4, of which 3 were waited for; matrix products, arithmetic and copies ran while one was open for 0% of the time, Pallas kernels for 3%

profile of v6, /device:TPU:0, one launch (start us, length us, event | category | flops | bytes accessed | tf_op | source)
XLA Modules:
  0.0 182.0 jit_solution(6989692237576004518)
XLA Ops:
  0.6 6.3 %shard_map.51 = bf16[32,32,2560]{2,1,0:T(8,128)(2,1)} custom-call(f32[32,81920]{1,0:T(8,128)} %in_hbm.1), custom_call_target="tpu_custom_call" | custom-call | tf_op jit(solution)/shard_map/pallas_call | solution.py:297
  6.9 0.0 copy-start.2
  6.9 0.0 copy-start.3
  7.0 7.4 %all-to-all-start = ((bf16[32,32,2560]{2,1,0:T(8,128)(2,1)}), bf16[32,32,2560]{2,1,0:T(8,128)(2,1)}, u32[]{:S(2)}, u32[]{:S(2)}) async-start(bf16[32,32,2560]{2,1,0:T(8,128)(2,1)} %shard_map.51), calls=%async_computation | async-start | bytes 10485760 | tf_op jit(solution)/shard_map/all_to_all | solution.py:310
  14.4 0.0 copy-done.2
  14.4 0.1 convert_element_type.8.refs_0_
  14.5 1.5 collective-permute-start.2
  16.0 0.4 collective-permute-start.1
  16.4 0.0 collective-permute-start
  16.4 0.0 copy-done.3
  16.5 0.2 broadcast_in_dim.2.places_ref
  16.7 0.1 pad_add_fusion.sources_ref
  16.7 54.8 %collective-permute-done.2.refs_3_ = bf16[256,1024]{1,0:T(8,128)(2,1)S(1)} collective-permute-done((bf16[256,1024]{1,0:T(8,128)(2,1)S(1)}, bf16[256,1024]{1,0:T(8,128)(2,1)S(1)}, u32[]{:S(2)}, u32[]{:S(2)}) %collective-permute-start.2) | collective-permute-done | bytes 524320 | tf_op jit(solution)/shard_map/ppermute | solution.py:274
  71.6 18.3 %collective-permute-done.1.refs_2_ = bf16[256,1024]{1,0:T(8,128)(2,1)S(1)} collective-permute-done((bf16[256,1024]{1,0:T(8,128)(2,1)S(1)}, bf16[256,1024]{1,0:T(8,128)(2,1)S(1)}, u32[]{:S(2)}, u32[]{:S(2)}) %collective-permute-start.1) | collective-permute-done | bytes 524320 | tf_op jit(solution)/shard_map/ppermute | solution.py:274
  89.9 0.0 collective-permute-done.refs_1_
  89.9 5.2 %shard_map.50 = (bf16[1024,1024]{1,0:T(8,128)(2,1)}, bf16[1024,1024]{1,0:T(8,128)(2,1)}, bf16[1024,1024]{1,0:T(8,128)(2,1)}) custom-call(s32[4]{0:T(128)S(1)} %pad_add_fusion.sources_ref, bf16[256,1024]{1,0:T(8,128)(2,1)S(1)} %convert_element_type.8.refs_0_, bf16[256,1024]{1,0:T(8,128)(2,1)S(1)} %collective-permute-done.refs_1_, ...), custom_call_target="tpu_custom_call" | custom-call | tf_op jit(solution)/shard_map/pallas_call | solution.py:317
  95.0 0.0 copy-start.1
  95.0 35.9 %all-to-all-done.w_hbm = bf16[32,32,2560]{2,1,0:T(8,128)(2,1)} async-done(((bf16[32,32,2560]{2,1,0:T(8,128)(2,1)}), bf16[32,32,2560]{2,1,0:T(8,128)(2,1)}, u32[]{:S(2)}, u32[]{:S(2)}) %all-to-all-start) | async-done | bytes 5242912 | tf_op jit(solution)/shard_map/all_to_all | solution.py:310
  131.0 9.3 %shard_map.52 = (f32[1024,2560]{1,0:T(8,128)S(1)}, f32[32,1,1152]{2,1,0:T(1,128)S(1)}) custom-call(s32[1024,128]{1,0:T(8,128)S(1)} %broadcast_in_dim.2.places_ref, s32[8,2560]{1,0:T(8,128)S(1)} %iota.9.columns_ref, bf16[1024,1024]{1,0:T(8,128)(2,1)} %get-tuple-element.16.x_hbm, bf16[32,32,2560]{2,1,0:T(8,128)(2,1)} %all-to-all-done.w_hbm), custom_call_target="tpu_custom_call" | custom-call | tf_op jit(solution)/shard_map/pallas_call | solution.py:336
  140.3 11.9 %all_to_all.15.got_ref = f32[32,1,1152]{2,1,0:T(1,128)S(1)} all-to-all(f32[32,1,1152]{2,1,0:T(1,128)S(1)} %get-tuple-element.17), channel_id=1, replica_groups=mesh['cls'=8,'row'=4] {'cls','row'}, dimensions={0} | all-to-all | bytes 294912 | tf_op jit(solution)/shard_map/all_to_all | solution.py:287
  152.2 0.0 copy-done.1
  152.2 0.0 copy-start
  152.2 8.2 %shard_map.53 = (bf16[1024,2560]{1,0:T(8,128)(2,1)S(1)}, f32[1024,2560]{1,0:T(8,128)S(1)}, f32[1,1024]{1,0:T(1,128)S(1)}, f32[32,1,2176]{2,1,0:T(1,128)S(1)}) custom-call(f32[32,1,1152]{2,1,0:T(1,128)S(1)} %all_to_all.15.got_ref, s32[1024,128]{1,0:T(8,128)S(1)} %broadcast_in_dim.2.places_ref, s32[8,2560]{1,0:T(8,128)S(1)} %iota.9.columns_ref, ...), custom_call_target="tpu_custom_call" | custom-call | tf_op jit(solution)/shard_map/pallas_call | solution.py:349
  160.4 13.0 %all_to_all.16.got_ref = f32[32,1,2176]{2,1,0:T(1,128)S(1)} all-to-all(f32[32,1,2176]{2,1,0:T(1,128)S(1)} %get-tuple-element.22), channel_id=1, replica_groups=mesh['cls'=8,'row'=4] {'cls','row'}, dimensions={0} | all-to-all | bytes 557056 | tf_op jit(solution)/shard_map/all_to_all | solution.py:287
  173.3 0.0 copy-done
  173.3 8.4 %shard_map.54 = (f32[1024,2560]{1,0:T(8,128)}, f32[2,1024]{1,0:T(2,128)}) custom-call(f32[1,1024]{1,0:T(1,128)S(1)} %get-tuple-element.21.norm_ref, f32[32,1,2176]{2,1,0:T(1,128)S(1)} %all_to_all.16.got_ref, s32[1024,128]{1,0:T(8,128)S(1)} %broadcast_in_dim.2.places_ref, s32[8,2560]{1,0:T(8,128)S(1)} %iota.9.columns_ref, bf16[1024,1024]{1,0:T(8,128)(2,1)S(1)} %copy-done, ...), custom_call_target="tpu_custom_call" | custom-call | tf_op jit(solution)/shard_map/pallas_call | solution.py:362
  (4 shorter events, 0.0 us)
Async XLA Ops:
  6.9 7.5 %copy-start.2 = (f32[256,1024]{1,0:T(8,128)S(1)}, f32[256,1024]{1,0:T(8,128)}, u32[]{:S(2)}) copy-start(f32[256,1024]{1,0:T(8,128)} %param.3) | copy-start | bytes 3145732
  6.9 9.5 %copy-start.3 = (s32[1024]{0:T(1024)S(1)}, s32[1024]{0:T(1024)}, u32[]{:S(2)}) copy-start(s32[1024]{0:T(1024)} %param.5) | copy-start | bytes 12292
  7.0 124.0 %all-to-all-start = ((bf16[32,32,2560]{2,1,0:T(8,128)(2,1)}), bf16[32,32,2560]{2,1,0:T(8,128)(2,1)}, u32[]{:S(2)}, u32[]{:S(2)}) async-start(bf16[32,32,2560]{2,1,0:T(8,128)(2,1)} %shard_map.51), calls=%async_computation | async-start | bytes 10485760 | tf_op jit(solution)/shard_map/all_to_all | solution.py:310
  14.5 57.1 %collective-permute-start.2 = (bf16[256,1024]{1,0:T(8,128)(2,1)S(1)}, bf16[256,1024]{1,0:T(8,128)(2,1)S(1)}, u32[]{:S(2)}, u32[]{:S(2)}) collective-permute-start(bf16[256,1024]{1,0:T(8,128)(2,1)S(1)} %convert_element_type.8.refs_0_), channel_id=1, source_target_pairs={{0,3},{1,2},{2,1},{3,0},{4,7},{5,6},{6,5},{7,4},{8,11},{9,10},{10,... | collective-permute-start | bytes 1572872 | tf_op jit(solution)/shard_map/ppermute | solution.py:274
  16.0 73.9 %collective-permute-start.1 = (bf16[256,1024]{1,0:T(8,128)(2,1)S(1)}, bf16[256,1024]{1,0:T(8,128)(2,1)S(1)}, u32[]{:S(2)}, u32[]{:S(2)}) collective-permute-start(bf16[256,1024]{1,0:T(8,128)(2,1)S(1)} %convert_element_type.8.refs_0_), channel_id=1, source_target_pairs={{0,2},{1,3},{2,0},{3,1},{4,6},{5,7},{6,4},{7,5},{8,10},{9,11},{10,... | collective-permute-start | bytes 1572872 | tf_op jit(solution)/shard_map/ppermute | solution.py:274
  16.4 73.5 %collective-permute-start = (bf16[256,1024]{1,0:T(8,128)(2,1)S(1)}, bf16[256,1024]{1,0:T(8,128)(2,1)S(1)}, u32[]{:S(2)}, u32[]{:S(2)}) collective-permute-start(bf16[256,1024]{1,0:T(8,128)(2,1)S(1)} %convert_element_type.8.refs_0_), channel_id=1, source_target_pairs={{0,1},{1,0},{2,3},{3,2},{4,5},{5,4},{6,7},{7,6},{8,9},{9,8},{10,11... | collective-permute-start | bytes 1572872 | tf_op jit(solution)/shard_map/ppermute | solution.py:274
  95.0 57.2 %copy-start.1 = (bf16[1024,1024]{1,0:T(8,128)(2,1)S(1)}, bf16[1024,1024]{1,0:T(8,128)(2,1)}, u32[]{:S(2)}) copy-start(bf16[1024,1024]{1,0:T(8,128)(2,1)} %get-tuple-element.19.gram_ref) | copy-start | bytes 6291460
  152.2 21.1 %copy-start = (bf16[1024,1024]{1,0:T(8,128)(2,1)S(1)}, bf16[1024,1024]{1,0:T(8,128)(2,1)}, u32[]{:S(2)}) copy-start(bf16[1024,1024]{1,0:T(8,128)(2,1)} %get-tuple-element.23.flipped_ref) | copy-start | bytes 6291460
